TPU v7x, 32 devices: a whole 2x2x4 slice. The times are simulated.
32 devices in a mesh: groups: 2 (over x), tile: 16 (over z, y, core).
Axes of the slice: x: 2, y: 2, z: 4, core: 2. Of those that a mesh axis runs over, the one named last changes fastest.
Arguments:
- tracer: float32 [32, 6, 8, 128, 128], P(('groups', 'tile')), parts along dimension 0, may hold values from -6 to 6
- courant_east: bfloat16 [32, 6, 8, 128, 128], P(('groups', 'tile')), parts along dimension 0, may hold values from -1.5 to 1.5
- courant_north: bfloat16 [32, 6, 8, 128, 128], P(('groups', 'tile')), parts along dimension 0, may hold values from -1.5 to 1.5
- diffusivity: bfloat16 [32, 6, 8, 128, 128], P(('groups', 'tile')), parts along dimension 0, may hold values from 0.049804688 to 5
- seam_table: int32 [6, 4, 3], replicated, may hold values from 0 to 5, as said below
Outputs:
- updated: float32 [32, 6, 8, 128, 128], P(('groups', 'tile')), parts along dimension 0
There are 2 independent parts, one for each index of `groups`. A program takes and returns all parts, laid end to end along the dimension named above; an argument that names none is the same for every part. Nothing has to cross between parts.
Inputs may be any that keep to these rules, and one draw needn't show every extreme that they name: seam_table[p, e] = (q, f, r) names the edge f of panel q != p that borders edge e of panel p, and r is 1 where their edge indices run in opposite directions, 0 otherwise; the 24 edges form 12 pairs whose entries name each other with the same r, as on the faces of a cube ; edge 3 of panel 0 borders edge 3 of panel 1.
All inputs are finite; a program needn't handle non-finite values.
Results may differ from a plain program's by a relative error of at most 0.0003.
Values sent between devices are 32-bit elements; how exact they have to be, the bound alone decides.
No kernel may reach another device: no remote copies, remote signals or barrier semaphores. Data moves between devices by JAX's collectives and lax.ppermute only.
A program may use at most 128 MiB of HBM per device.

v0:
```python
import math

import jax
import jax.numpy as jnp
from jax import lax
from jax.sharding import PartitionSpec as P

DEPTH = 2


def padded(block, sides, width):
    for axis, dim in sides:
        count = lax.axis_size(axis)
        forward = [(i, i + 1) for i in range(count - 1)]
        forward.append((count - 1, 0))
        backward = [(target, source) for source, target in forward]
        low = lax.ppermute(
            lax.slice_in_dim(block, block.shape[dim] - width, None, axis=dim), axis, forward
        )
        high = lax.ppermute(lax.slice_in_dim(block, 0, width, axis=dim), axis, backward)
        block = jnp.concatenate([low, block, high], axis=dim)
    return block


def from_behind(value, axis, steps):
    count = lax.axis_size(axis)
    pairs = [(source, (source + steps) % count) for source in range(count)]
    return lax.ppermute(value, axis, pairs)


def edge_strips(panels, rows_deep):
    south_rows = jnp.moveaxis(panels[:, :, :, :rows_deep], 3, 1)
    east_rows = jnp.moveaxis(panels[:, :, ::-1, :][:, :, :rows_deep, :], 2, 1)
    north_rows = jnp.moveaxis(panels[:, :, :, ::-1][:, :, :, :rows_deep], 3, 1)
    west_rows = jnp.moveaxis(panels[:, :, :rows_deep, :], 2, 1)
    return jnp.stack([south_rows, east_rows, north_rows, west_rows], axis=1)


def centered(extended, along):
    kept = extended.shape[along] - 4

    def shifted(offset):
        return lax.slice_in_dim(extended, 2 + offset, 2 + offset + kept, axis=along)

    return (8.0 * (shifted(1) - shifted(-1)) - (shifted(2) - shifted(-2))) / 12.0


def advance(panels, ghosts, courant_east, courant_north, diffusivity):
    west_part = jnp.moveaxis(ghosts[:, 3, ::-1], 1, 2)
    east_part = jnp.moveaxis(ghosts[:, 1], 1, 2)
    south_part = jnp.transpose(ghosts[:, 0, ::-1], (0, 2, 3, 1))
    north_part = jnp.transpose(ghosts[:, 2], (0, 2, 3, 1))
    along_first = jnp.concatenate([west_part, panels, east_part], axis=2)
    along_second = jnp.concatenate([south_part, panels, north_part], axis=3)
    forced = panels - (
        courant_east.astype(jnp.float32) * centered(along_first, 2)
        + courant_north.astype(jnp.float32) * centered(along_second, 3)
    )
    coupling = diffusivity.astype(jnp.float32)
    ratios = []
    partial_values = []
    for height in range(panels.shape[1]):
        diagonal = 1.0 + coupling[:, height]
        if height > 0:
            below = coupling[:, height - 1]
            pivot_value = diagonal + below - below * ratios[-1]
            current = (forced[:, height] + below * partial_values[-1]) / pivot_value
        else:
            pivot_value = diagonal
            current = forced[:, height] / pivot_value
        ratios.append(coupling[:, height] / pivot_value)
        partial_values.append(current)
    solved = [partial_values[-1]]
    for height in range(panels.shape[1] - 2, -1, -1):
        solved.insert(0, partial_values[height] + ratios[height] * solved[0])
    return jnp.stack(solved, axis=1)


def panel_tiles(device, across):
    total = across * across
    tile_offset = jnp.arange(6, dtype=jnp.int32) % 2 * (total // 2 + 1)
    return ((device - tile_offset) % total, tile_offset)


def placement(device, across):
    panel_tile, tile_offset = panel_tiles(device, across)
    row_no = panel_tile // across
    col_no = panel_tile % across
    on_edge = jnp.stack(
        [col_no == 0, row_no == across - 1, col_no == across - 1, row_no == 0], axis=1
    ).reshape(24)
    along_edge = jnp.stack([row_no, col_no, row_no, col_no], axis=1).reshape(24)
    return (on_edge, along_edge, panel_tile, tile_offset)


def device_at(edge_no, spot, across):
    return jnp.where(
        edge_no == 0,
        spot * across,
        jnp.where(
            edge_no == 1,
            (across - 1) * across + spot,
            jnp.where(edge_no == 2, spot * across + across - 1, spot),
        ),
    )


def neighbour_step(edge_no, across):
    return jnp.where(
        edge_no == 0, -1, jnp.where(edge_no == 1, across, jnp.where(edge_no == 2, 1, -across))
    )


def sources(seam_table, own_device, across):
    total = across * across
    on_edge, along_edge, panel_tile, tile_offset = placement(own_device, across)
    flat_table = seam_table.reshape(24, 3)
    ghost_edge = jnp.arange(24, dtype=jnp.int32) % 4
    ghost_panel = jnp.arange(24, dtype=jnp.int32) // 4
    turned_spot = jnp.where(flat_table[:, 2] == 1, across - 1 - along_edge, along_edge)
    far_tile = device_at(flat_table[:, 1], turned_spot, across)
    far_device = (far_tile + jnp.take(tile_offset, flat_table[:, 0])) % total
    near_device = (own_device + neighbour_step(ghost_edge, across)) % total
    source_device = jnp.where(on_edge, far_device, near_device)
    source_block = jnp.where(
        on_edge, flat_table[:, 0] * 4 + flat_table[:, 1], ghost_panel * 4 + (ghost_edge + 2) % 4
    )
    reverse_it = jnp.logical_and(on_edge, flat_table[:, 2] == 1)
    return (on_edge, flat_table, source_device, source_block, reverse_it, panel_tile)


def shards(tracer, courant_east, courant_north, diffusivity, seam_table):
    panels = tracer[0]
    tile_count = lax.axis_size("tile")
    across = math.isqrt(tile_count)
    own_device = lax.axis_index("tile")
    strips = edge_strips(panels, DEPTH)
    blocks = strips.reshape((24,) + strips.shape[2:])
    on_edge, flat_table, source_device, source_block, reverse_it, panel_tile = sources(
        seam_table, own_device, across
    )
    row_no = panel_tile // across
    col_no = panel_tile % across
    side_first = jnp.where(col_no == across - 1, 2, 0).astype(jnp.int32)
    side_second = jnp.where(row_no == 0, 3, 1).astype(jnp.int32)
    first_rows = jnp.take_along_axis(strips, side_first[:, None, None, None, None], axis=1)[:, 0]
    second_rows = jnp.take_along_axis(strips, side_second[:, None, None, None, None], axis=1)[:, 0]
    packed = jnp.concatenate([first_rows, second_rows], axis=0)
    collected = lax.all_gather(packed[None], "tile", axis=0, tiled=True)
    slot_in = jnp.where(flat_table[:, 1] % 2 == 0, 0, 6) + flat_table[:, 0]
    picked = jnp.take(
        collected.reshape((tile_count * 12,) + blocks.shape[1:]),
        source_device * 12 + slot_in,
        axis=0,
        mode="clip",
    )
    picked = jnp.where(reverse_it[:, None, None, None], picked[..., ::-1], picked)
    both_rows = jnp.stack([strips[:, 0], strips[:, 2]], axis=0)
    widened = padded(both_rows, (("tile", 0),), 1)
    from_west = from_behind(strips[:, 1], "tile", across)
    from_east = from_behind(strips[:, 3], "tile", -across)
    inside = jnp.stack([widened[0], from_east, widened[3], from_west], axis=1).reshape(blocks.shape)
    ghosts = jnp.where(on_edge[:, None, None, None], picked, inside)
    updated = advance(
        panels, ghosts.reshape(strips.shape), courant_east[0], courant_north[0], diffusivity[0]
    )
    return updated[None]


def solution(mesh):
    placed = (
        P(("groups", "tile"), None, None, None, None),
        P(("groups", "tile"), None, None, None, None),
        P(("groups", "tile"), None, None, None, None),
        P(("groups", "tile"), None, None, None, None),
        P(),
    )
    return jax.shard_map(
        shards,
        mesh=mesh,
        in_specs=placed,
        out_specs=P(("groups", "tile"), None, None, None, None),
        check_vma=False,
    )
```

profile of v0, /device:TPU:0, one launch (start us, length us, event | category | flops | bytes accessed | tf_op | source)
XLA Modules:
  0.0 114.8 jit_solution(10395726204144280213)
XLA Ops:
  6.5 0.0 all-gather.3.cloned.1.call-start
  6.6 1.1 slice_bitcast_fusion
  7.7 5.5 %fusion.60 = (f32[6,8,128,2]{3,2,1,0:T(8,128)}, f32[6,8,128,2]{3,2,1,0:T(8,128)S(1)}) fusion(f32[6,8,128,128]{3,2,1,0:T(8,128)} %bitcast.97), kind=kLoop, calls=%fused_computation.177 | loop fusion | bytes 196608 | tf_op jit(solution)/shard_map/slice | solution.py:34
  13.2 0.1 slice.139
  13.3 2.4 %copy.55 = f32[6,8,128,2]{2,3,1,0:T(2,128)S(1)} copy(f32[6,8,128,2]{3,2,1,0:T(8,128)} %get-tuple-element.24) | data formatting | bytes 98304
  15.7 0.0 copy-start.4
  15.7 0.1 slice.141
  15.8 1.2 %copy.54 = f32[6,8,128,2]{2,3,1,0:T(2,128)S(1)} copy(f32[6,8,128,2]{3,2,1,0:T(8,128)S(1)} %get-tuple-element.25) | data formatting | bytes 98304
  17.0 0.0 copy-start.2
  17.0 0.1 pad_maximum_fusion.4
  17.1 0.6 gather_fusion.3
  17.7 0.6 gather_fusion.2
  18.4 0.1 fusion.28
  18.4 0.1 fusion.27
  18.6 0.7 copy.44
  19.2 0.0 all-gather.3.cloned.1.call-update
  19.3 3.1 %collective-permute-start.3 = (f32[6,2,8,128]{3,1,2,0:T(2,128)S(1)}, f32[6,2,8,128]{3,1,2,0:T(2,128)S(1)}, u32[]{:S(2)}, u32[]{:S(2)}) collective-permute-start(f32[6,2,8,128]{3,1,2,0:T(2,128)S(1)} %bitcast.107), channel_id=1, source_target_pairs={{0,4},{1,5},{2,6},{3,7},{4,8},{5,9},{6,10},{7,11},{8,12},{9,13},{1... | collective-permute-start | bytes 147464 | tf_op jit(solution)/shard_map/ppermute | solution.py:28
  22.4 2.1 %collective-permute-start.1 = (f32[6,2,8,128]{3,1,2,0:T(2,128)S(1)}, f32[6,2,8,128]{3,1,2,0:T(2,128)S(1)}, u32[]{:S(2)}, u32[]{:S(2)}) collective-permute-start(f32[6,2,8,128]{3,1,2,0:T(2,128)S(1)} %get-tuple-element.22), channel_id=1, source_target_pairs={{0,12},{1,13},{2,14},{3,15},{4,0},{5,1},{6,2},{7,3},{8,4},{9,5},{1... | collective-permute-start | bytes 147464 | tf_op jit(solution)/shard_map/ppermute | solution.py:28
  24.5 0.0 collective-permute-start
  24.5 4.4 %collective-permute-start.2 = (f32[1,6,2,8,128]{4,3,2,1,0:T(8,128)S(1)}, f32[1,6,2,8,128]{4,3,2,1,0:T(8,128)S(1)}, u32[]{:S(2)}, u32[]{:S(2)}) collective-permute-start(f32[1,6,2,8,128]{4,3,2,1,0:T(8,128)S(1)} %copy.47), channel_id=1, source_target_pairs={{1,0},{2,1},{3,2},{4,3},{5,4},{6,5},{7,6},{8,7},{9,8},{10,9},{11,1... | collective-permute-start | bytes 147464 | tf_op jit(solution)/shard_map/ppermute | solution.py:20
  29.0 0.1 pad_add_fusion.1
  29.1 0.1 broadcast_in_dim.51
  29.1 0.1 reshape.440
  29.3 0.1 pad_add_fusion
  29.3 0.1 reshape.441
  29.4 0.0 copy-done.4
  29.4 0.1 copy.41
  29.5 0.1 reshape.438
  29.6 0.7 gather_fusion
  30.4 0.0 copy-done.2
  30.4 2.0 %bitcast_convert_fusion = f32[6,8,128,128]{3,2,1,0:T(8,128)} fusion(bf16[1,6,8,128,128]{4,3,2,1,0:T(8,128)(2,1)S(1)} %copy-done.2), kind=kLoop, calls=%fused_computation.34 | loop fusion | flops 786432 | bytes 4718592 | tf_op jit(solution)/shard_map/convert_element_type | solution.py:59
  32.4 0.0 collective-permute-done
  32.5 0.0 collective-permute-done.2
  32.5 0.0 collective-permute-done.3
  32.5 0.0 collective-permute-done.1
  32.5 0.1 pad_maximum_fusion.5
  32.7 29.1 %all-gather.3.cloned.1.call-done = f32[192,2,8,128]{3,2,1,0:T(8,128)} async-done(((f32[12,2,8,128]{3,2,1,0:T(8,128)}), f32[192,2,8,128]{3,2,1,0:T(8,128)}) %all-gather.3.cloned.1.call-update) | async-done | bytes 1572880 | tf_op jit(solution)/shard_map/all_gather | solution.py:149
  61.8 2.0 %gather_fusion.1 = f32[24,2,8,128]{3,2,1,0:T(8,128)S(1)} fusion(f32[192,2,8,128]{3,2,1,0:T(8,128)} %all-gather.3.cloned.1.call-done, s32[1024]{0:T(1024)S(1)} %pad_clamp_fusion), kind=kCustom, calls=%fused_computation.3 | custom fusion | bytes 393312 | tf_op jit(solution)/shard_map/jit(_take)/gather | solution.py:151
  63.7 0.1 rev.11
  63.8 0.1 bitcast_select_fusion
  64.0 0.1 rev.12
  64.2 2.2 %copy.58 = f32[6,1,2,8,128]{2,4,3,0,1:T(8,128)} copy(f32[6,1,2,8,128]{4,3,2,1,0:T(8,128)S(1)} %get-tuple-element.26) | data formatting | bytes 98304
  66.4 2.3 %copy.59 = f32[6,1,2,8,128]{2,4,3,0,1:T(8,128)} copy(f32[6,1,2,8,128]{4,3,2,1,0:T(8,128)S(1)} %get-tuple-element.29) | data formatting | bytes 98304
  68.7 0.0 copy-start
  68.7 26.0 %rev.13 = f32[6,1,2,8,128]{2,4,3,0,1:T(8,128)} reverse(f32[6,1,2,8,128]{2,4,3,0,1:T(8,128)} %copy.59), dimensions={2} | reverse | bytes 98304 | tf_op jit(solution)/shard_map/rev | solution.py:51
  94.6 0.0 copy-done
  94.6 0.0 copy-start.1
  94.6 9.8 %fusion.7 = f32[6,8,128,128]{3,2,1,0:T(8,128)S(1)} fusion(f32[6,8,128,128]{3,2,1,0:T(8,128)S(1)} %bitcast.98, f32[6,8,2,128]{3,2,1,0:T(2,128)S(1)} %bitcast.110, f32[6,8,2,128]{3,2,1,0:T(2,128)S(1)} %bitcast.111, f32[6,8,128,2]{3,2,1,0:T(8,128)} %bitcast.100, f32[6,8,128,2]{3,2,1,0:T(8,128)} %bitcast.99, bf16[1,6,8,128,128]{4,3,2,1,0:T(8,128)(2,1)} %param.9, ...), kind=kLoop, calls=%fused_computation.19 | loop fusion | flops 18874368 | bytes 9633792 | tf_op jit(solution)/shard_map/sub | solution.py:55
  104.5 0.0 copy-done.1
  104.5 0.7 fusion.22
  105.2 0.7 add_dynamic-update-slice_fusion
  105.9 0.1 constant_dynamic-update-slice_fusion.5
  106.0 0.1 constant_dynamic-update-slice_fusion.3
  106.1 0.1 constant_dynamic-update-slice_fusion.1
  106.2 0.0 copy-start.3
  106.3 1.7 %copy-done.3 = f32[6,8,128,128]{3,2,1,0:T(8,128)} copy-done((f32[6,8,128,128]{3,2,1,0:T(8,128)}, f32[6,8,128,128]{3,2,1,0:T(8,128)S(1)}, u32[]{:S(2)}) %copy-start.3) | copy-done | bytes 3145752
  (28 shorter events, 0.5 us)
Async XLA Ops:
  6.5 55.2 %all-gather.3.cloned.1.call-start = ((), (), s32[]{:S(2)}) async-start(), calls=%async_computation | async-start | bytes 1671168 | tf_op jit(solution)/shard_map/all_gather | solution.py:149
  15.7 13.8 %copy-start.4 = (s32[6,4,3]{0,1,2:T(4,128)S(1)}, s32[6,4,3]{0,1,2:T(4,128)}, u32[]{:S(2)}) copy-start(s32[6,4,3]{0,1,2:T(4,128)} %param.11) | copy-start | bytes 868
  17.0 13.4 %copy-start.2 = (bf16[1,6,8,128,128]{4,3,2,1,0:T(8,128)(2,1)S(1)}, bf16[1,6,8,128,128]{4,3,2,1,0:T(8,128)(2,1)}, u32[]{:S(2)}) copy-start(bf16[1,6,8,128,128]{4,3,2,1,0:T(8,128)(2,1)} %param.10) | copy-start | bytes 4718596
  19.3 13.2 %collective-permute-start.3 = (f32[6,2,8,128]{3,1,2,0:T(2,128)S(1)}, f32[6,2,8,128]{3,1,2,0:T(2,128)S(1)}, u32[]{:S(2)}, u32[]{:S(2)}) collective-permute-start(f32[6,2,8,128]{3,1,2,0:T(2,128)S(1)} %bitcast.107), channel_id=1, source_target_pairs={{0,4},{1,5},{2,6},{3,7},{4,8},{5,9},{6,10},{7,11},{8,12},{9,13},{1... | collective-permute-start | bytes 147464 | tf_op jit(solution)/shard_map/ppermute | solution.py:28
  22.4 10.1 %collective-permute-start.1 = (f32[6,2,8,128]{3,1,2,0:T(2,128)S(1)}, f32[6,2,8,128]{3,1,2,0:T(2,128)S(1)}, u32[]{:S(2)}, u32[]{:S(2)}) collective-permute-start(f32[6,2,8,128]{3,1,2,0:T(2,128)S(1)} %get-tuple-element.22), channel_id=1, source_target_pairs={{0,12},{1,13},{2,14},{3,15},{4,0},{5,1},{6,2},{7,3},{8,4},{9,5},{1... | collective-permute-start | bytes 147464 | tf_op jit(solution)/shard_map/ppermute | solution.py:28
  24.5 8.0 %collective-permute-start = (f32[1,6,2,8,128]{4,3,2,1,0:T(8,128)S(1)}, f32[1,6,2,8,128]{4,3,2,1,0:T(8,128)S(1)}, u32[]{:S(2)}, u32[]{:S(2)}) collective-permute-start(f32[1,6,2,8,128]{4,3,2,1,0:T(8,128)S(1)} %copy.45), channel_id=1, source_target_pairs={{0,1},{1,2},{2,3},{3,4},{4,5},{5,6},{6,7},{7,8},{8,9},{9,10},{10,1... | collective-permute-start | bytes 147464 | tf_op jit(solution)/shard_map/ppermute | solution.py:17
  24.5 8.0 %collective-permute-start.2 = (f32[1,6,2,8,128]{4,3,2,1,0:T(8,128)S(1)}, f32[1,6,2,8,128]{4,3,2,1,0:T(8,128)S(1)}, u32[]{:S(2)}, u32[]{:S(2)}) collective-permute-start(f32[1,6,2,8,128]{4,3,2,1,0:T(8,128)S(1)} %copy.47), channel_id=1, source_target_pairs={{1,0},{2,1},{3,2},{4,3},{5,4},{6,5},{7,6},{8,7},{9,8},{10,9},{11,1... | collective-permute-start | bytes 147464 | tf_op jit(solution)/shard_map/ppermute | solution.py:20
  68.7 26.0 %copy-start = (f32[1,6,8,128,128]{4,3,2,1,0:T(8,128)S(1)}, f32[1,6,8,128,128]{4,3,2,1,0:T(8,128)}, u32[]{:S(2)}) copy-start(f32[1,6,8,128,128]{4,3,2,1,0:T(8,128)} %param.7) | copy-start | bytes 9437188
  94.6 9.9 %copy-start.1 = (f32[6,8,128,128]{3,2,1,0:T(8,128)S(1)}, f32[6,8,128,128]{3,2,1,0:T(8,128)}, u32[]{:S(2)}) copy-start(f32[6,8,128,128]{3,2,1,0:T(8,128)} %bitcast_convert_fusion) | copy-start | bytes 9437188
  106.2 1.7 %copy-start.3 = (f32[6,8,128,128]{3,2,1,0:T(8,128)}, f32[6,8,128,128]{3,2,1,0:T(8,128)S(1)}, u32[]{:S(2)}) copy-start(f32[6,8,128,128]{3,2,1,0:T(8,128)S(1)} %constant_dynamic-update-slice_fusion) | copy-start | bytes 9437188
Sparse Core Ops, SparseCore 0:
  19.4 42.3 all-gather.2
where the time goes:
time: 117 us; the launch traced here: 115 us
  local copies, waits for them, and re-layouts  48 us (41%)
  waiting for transfers between devices  29.1 us (25%)
  other arithmetic  14.3 us (12%)
  between operations  13.7 us (12%)
  starting transfers between devices  9.64 us (8%)
    all_gather x1, waiting for transfers between devices, shards(): collected = lax.all_gather(packed[None], 'tile', axis=0, tiled=True)  29.1 us
    rev x1, local copies, waits for them, and re-layouts, advance(): south_part = jnp.transpose(ghosts[:, 0, ::-1], (0, 2, 3, 1))  26 us
    unnamed x20, local copies, waits for them, and re-layouts  9.93 us
    sub x1, other arithmetic, advance(): panels - (courant_east.astype(jnp.float32) * centered(along_first, 2) + c...  9.84 us
    slice x2, local copies, waits for them, and re-layouts, edge_strips(): north_rows = jnp.moveaxis(panels[:, :, :, ::-1][:, :, :, :rows_deep], 3, 1)  5.6 us
    ppermute x2, starting transfers between devices, from_behind(): return lax.ppermute(value, axis, pairs)  5.2 us
    ppermute x1, starting transfers between devices, padded(): lax.ppermute(lax.slice_in_dim(block, 0, width, axis=dim), axis, backward)  4.44 us
  transfers between devices with their start and end apart: 5, of which 1 were waited for; matrix products, arithmetic and copies ran while one was open for 3% of the time, Pallas kernels for 0%

commit v1 on v0

v1 whole, which is shorter than its diff:
```python
import math

import jax
import jax.numpy as jnp
from jax import lax
from jax.experimental import pallas as pl
from jax.experimental.pallas import tpu as pltpu
from jax.sharding import PartitionSpec as P

DEPTH = 2


def split3(x):
    hi = x.astype(jnp.bfloat16)
    rest = x - hi.astype(jnp.float32)
    mid = rest.astype(jnp.bfloat16)
    low = (rest - mid.astype(jnp.float32)).astype(jnp.bfloat16)
    return hi, mid, low


def pack_body(tracer_ref, out_ref, *, levels, cells):
    panel = pl.program_id(0)
    lane = lax.broadcasted_iota(jnp.int32, (cells, cells), 1)
    group = lane // (2 * DEPTH)
    packed = jnp.zeros((cells, cells), jnp.float32)
    for k in range(levels):
        turned = pltpu.roll(tracer_ref[0, k], 2 * DEPTH * k + DEPTH, 1)
        packed = jnp.where(group == k, turned, packed)
    rows = packed.T
    for k in range(levels):
        for d in range(DEPTH):
            m = k * DEPTH + d
            south = 2 * DEPTH * k + DEPTH + d
            north = 2 * DEPTH * k + DEPTH - 1 - d
            out_ref[m, pl.ds(panel * 4, 1), :] = rows[south : south + 1]
            out_ref[m, pl.ds(panel * 4 + 1, 1), :] = tracer_ref[0, k, cells - 1 - d : cells - d, :]
            out_ref[m, pl.ds(panel * 4 + 2, 1), :] = rows[north : north + 1]
            out_ref[m, pl.ds(panel * 4 + 3, 1), :] = tracer_ref[0, k, d : d + 1, :]


def pack(panels):
    count, levels, cells, _ = panels.shape
    return pl.pallas_call(
        lambda a, o: pack_body(a, o, levels=levels, cells=cells),
        grid=(count,),
        in_specs=[pl.BlockSpec((1, levels, cells, cells), lambda p: (p, 0, 0, 0))],
        out_specs=pl.BlockSpec((levels * DEPTH, count * 4, cells), lambda p: (0, 0, 0)),
        out_shape=jax.ShapeDtypeStruct((levels * DEPTH, count * 4, cells), jnp.float32),
        name="pack",
    )(panels)


def route_body(index_ref, rows_ref, out_ref):
    total, cells = rows_ref.shape
    source = lax.broadcasted_iota(jnp.int32, (cells, cells), 0)
    target = lax.broadcasted_iota(jnp.int32, (cells, cells), 1)
    flip = (source + target == cells - 1).astype(jnp.float32).astype(jnp.bfloat16)
    parts = split3(rows_ref[...])
    flipped = [
        jnp.dot(part, flip, preferred_element_type=jnp.float32).astype(jnp.bfloat16)
        for part in parts
    ]
    both = jnp.concatenate(
        [jnp.concatenate(parts, axis=1), jnp.concatenate(flipped, axis=1)], axis=0
    )
    numbers = lax.broadcasted_iota(jnp.int32, (2 * total, index_ref.shape[1]), 0)
    width = index_ref.shape[1]
    for c in range(index_ref.shape[0]):
        chosen = (numbers == index_ref[c : c + 1, :]).astype(jnp.float32).astype(jnp.bfloat16)
        got = lax.dot_general(
            chosen, both, (((0,), (0,)), ((), ())), preferred_element_type=jnp.float32
        )
        out_ref[c * width : (c + 1) * width, :] = (
            got[:, :cells] + got[:, cells : 2 * cells]
        ) + got[:, 2 * cells :]


def route(index, rows):
    return pl.pallas_call(
        route_body,
        out_shape=jax.ShapeDtypeStruct(rows.shape, rows.dtype),
        name="route",
    )(index, rows)


def advance_body(
    tracer_ref, east_ref, north_ref, diff_ref, own_ref, ghost_ref, out_ref, ext_ref, fix_ref,
    *, levels, cells, step,
):
    panel = pl.program_id(0)
    rows = levels * DEPTH

    def strip(ref, edge):
        return ref[0:rows, pl.ds(panel * 4 + edge, 1), :].reshape(rows, cells)

    south = strip(ghost_ref, 0) - strip(own_ref, 2)
    north = strip(ghost_ref, 2) - strip(own_ref, 0)
    parts = [part.astype(jnp.float32) for side in (south, north) for part in split3(side)]
    stacked = jnp.concatenate(parts, axis=0)
    depth_of = lax.broadcasted_iota(jnp.int32, (rows, cells), 0) % DEPTH
    level_of = lax.broadcasted_iota(jnp.int32, (rows, cells), 0) // DEPTH
    lane = lax.broadcasted_iota(jnp.int32, (rows, cells), 1)
    from_south = jnp.where(
        depth_of == 0,
        jnp.where(lane == 0, -8.0, jnp.where(lane == 1, 1.0, 0.0)),
        jnp.where(lane == 0, 1.0, 0.0),
    )
    from_north = jnp.where(
        depth_of == 0,
        jnp.where(lane == cells - 1, 8.0, jnp.where(lane == cells - 2, -1.0, 0.0)),
        jnp.where(lane == cells - 1, -1.0, 0.0),
    )
    spread = jnp.concatenate([from_south] * 3 + [from_north] * 3, axis=0)
    levels_stacked = jnp.concatenate([level_of] * 6, axis=0)
    spread_all = jnp.concatenate(
        [jnp.where(levels_stacked == k, spread, 0.0) for k in range(levels)], axis=1
    ).astype(jnp.bfloat16)
    fix_ref[...] = jnp.dot(
        stacked.T.astype(jnp.bfloat16), spread_all, preferred_element_type=jnp.float32
    )

    for k in range(levels):
        ext_ref[k, 8 : 8 + cells, :] = tracer_ref[0, k]
        for d in range(DEPTH):
            m = k * DEPTH + d
            ext_ref[k, 7 - d : 8 - d, :] = ghost_ref[m, pl.ds(panel * 4 + 3, 1), :]
            ext_ref[k, 8 + cells + d : 9 + cells + d, :] = ghost_ref[
                m, pl.ds(panel * 4 + 1, 1), :
            ]

    for start in range(0, cells, step):
        ratios = []
        partial_values = []
        below = None
        for k in range(levels):

            def shifted(offset):
                return ext_ref[k, 8 + start + offset : 8 + start + offset + step, :]

            q = tracer_ref[0, k, start : start + step, :]
            along_first = 8.0 * (shifted(1) - shifted(-1)) - (shifted(2) - shifted(-2))
            along_second = (
                8.0 * (pltpu.roll(q, cells - 1, 1) - pltpu.roll(q, 1, 1))
                - (pltpu.roll(q, cells - 2, 1) - pltpu.roll(q, 2, 1))
            ) + fix_ref[start : start + step, k * cells : (k + 1) * cells]
            east = east_ref[0, k, start : start + step, :].astype(jnp.float32)
            north_c = north_ref[0, k, start : start + step, :].astype(jnp.float32)
            forced = q - (east * along_first + north_c * along_second) * (1.0 / 12.0)
            coupling = diff_ref[0, k, start : start + step, :].astype(jnp.float32)
            pivot = 1.0 + coupling
            if k > 0:
                pivot = pivot + below - below * ratios[-1]
                forced = forced + below * partial_values[-1]
            inverse = 1.0 / pivot
            ratios.append(coupling * inverse)
            partial_values.append(forced * inverse)
            below = coupling
        value = partial_values[-1]
        out_ref[0, levels - 1, start : start + step, :] = value
        for k in range(levels - 2, -1, -1):
            value = partial_values[k] + ratios[k] * value
            out_ref[0, k, start : start + step, :] = value


def advance(panels, east, north, diff, own, ghosts):
    count, levels, cells, _ = panels.shape
    block = pl.BlockSpec((1, levels, cells, cells), lambda p: (p, 0, 0, 0))
    own_whole = pl.BlockSpec(own.shape, lambda p: (0, 0, 0))
    ghost_whole = pl.BlockSpec((levels * DEPTH,) + ghosts.shape[1:], lambda p: (0, 0, 0))
    return pl.pallas_call(
        lambda *refs: advance_body(*refs, levels=levels, cells=cells, step=16),
        grid=(count,),
        in_specs=[block, block, block, block, own_whole, ghost_whole],
        out_specs=block,
        out_shape=jax.ShapeDtypeStruct(panels.shape, panels.dtype),
        scratch_shapes=[
            pltpu.VMEM((levels, cells + 16, cells), jnp.float32),
            pltpu.VMEM((cells, levels * cells), jnp.float32),
        ],
        name="advance",
    )(panels, east, north, diff, own, ghosts)


def row_sources(seam_table, across):
    total = across * across
    device = jnp.arange(total, dtype=jnp.int32)[:, None]
    slot = jnp.arange(24, dtype=jnp.int32)[None, :]
    panel = slot // 4
    edge = slot % 4
    flat = seam_table.reshape(24, 3)
    far_panel = flat[:, 0][None, :]
    far_edge = flat[:, 1][None, :]
    turned = flat[:, 2][None, :] == 1
    shift = total // 2 + 1
    tile = (device - panel % 2 * shift) % total
    row = tile // across
    col = tile % across
    last = across - 1
    on_edge = jnp.where(
        edge == 0, col == 0, jnp.where(edge == 1, row == last, jnp.where(edge == 2, col == last, row == 0))
    )
    along = jnp.where(edge % 2 == 0, row, col)
    spot = jnp.where(turned, last - along, along)
    far_tile = jnp.where(
        far_edge == 0,
        spot * across,
        jnp.where(far_edge == 1, last * across + spot, jnp.where(far_edge == 2, spot * across + last, spot)),
    )
    far_device = (far_tile + far_panel % 2 * shift) % total
    step = jnp.where(edge == 0, -1, jnp.where(edge == 1, across, jnp.where(edge == 2, 1, -across)))
    near_device = (device + step) % total
    source = jnp.where(
        on_edge,
        far_device * 24 + far_panel * 4 + far_edge,
        near_device * 24 + panel * 4 + (edge + 2) % 4,
    )
    return source + jnp.where(on_edge & turned, total * 24, 0)


def shards(tracer, courant_east, courant_north, diffusivity, seam_table):
    panels = tracer[0]
    tile_count = lax.axis_size("tile")
    across = math.isqrt(tile_count)
    cells = panels.shape[-1]
    own = pack(panels)
    rows = own.shape[0]
    assert tile_count >= rows
    send = own
    if tile_count > rows:
        send = jnp.pad(own, ((0, tile_count - rows), (0, 0), (0, 0)))
    held = lax.all_to_all(send, "tile", 0, 0, tiled=True)
    index = row_sources(seam_table, across).reshape(-1, cells)
    routed = route(index, held.reshape(-1, cells))
    ghosts = lax.all_to_all(routed.reshape(held.shape), "tile", 0, 0, tiled=True)
    updated = advance(
        panels, courant_east[0], courant_north[0], diffusivity[0], own, ghosts
    )
    return updated[None]


def solution(mesh):
    placed = P(("groups", "tile"), None, None, None, None)
    return jax.shard_map(
        shards,
        mesh=mesh,
        in_specs=(placed, placed, placed, placed, P()),
        out_specs=placed,
        check_vma=False,
    )
```

time: 117 us -> 46.2 us (0.39); the launches traced: 115 us -> 45.7 us
  local copies, waits for them, and re-layouts: 48 us -> 2.27 us
  waiting for transfers between devices: 29.1 us -> 6.45 us
  Pallas kernels: 0 us -> 15.5 us
  other arithmetic: 14.3 us -> 0.71 us
  between operations: 13.7 us -> 0.22 us
  blocking collectives: 0 us -> 13.1 us
  starting transfers between devices: 9.64 us -> 7.41 us
    all_gather x1 -> x0, waiting for transfers between devices: 29.1 us -> none  [shards(): collected = lax.all_gather(packed[None], 'tile', axis=0, tiled=True)]
    rev x3 -> x0, local copies, waits for them, and re-layouts: 26.2 us -> none  [the longest x1 26 us: advance(): south_part = jnp.transpose(ghosts[:, 0, ::-1], (0, 2, 3, 1))]
    pallas_call x0 -> x3, Pallas kernels: none -> 15.5 us  [the longest x1 8.38 us: advance(): pl.pallas_call(lambda *refs: advance_body(*refs, levels=levels, cells=cel...]
    all_to_all x0 -> x1, blocking collectives: none -> 13.1 us  [shards(): lax.all_to_all(routed.reshape(held.shape), 'tile', 0, 0, tiled=True)]
    sub x1, other arithmetic: 9.84 us -> 0.01 us  [row_sources(): tile = (device - panel % 2 * shift) % total]
    ppermute x4 -> x0, starting transfers between devices: 9.63 us -> none  [the longest x2 5.2 us: from_behind(): return lax.ppermute(value, axis, pairs)]
    unnamed x20 -> x5, local copies, waits for them, and re-layouts: 9.93 us -> 0.79 us
    all_to_all x0 -> x1, starting transfers between devices: none -> 7.41 us  [shards(): held = lax.all_to_all(send, 'tile', 0, 0, tiled=True)]
  transfers between devices with their start and end apart: 5 -> 1, of which waited for: 1 -> 1; matrix products, arithmetic and copies ran while one was open for 3% -> 5% of each run, Pallas kernels for 0% -> 0%
where the time goes in v1:
time: 46.2 us; the launch traced here: 45.7 us
  Pallas kernels  15.5 us (34%)
  blocking collectives  13.1 us (28%)
  starting transfers between devices  7.41 us (16%)
  waiting for transfers between devices  6.45 us (14%)
  local copies, waits for them, and re-layouts  2.27 us (5%)
  other arithmetic  0.71 us (2%)
    all_to_all x1, blocking collectives, shards(): lax.all_to_all(routed.reshape(held.shape), 'tile', 0, 0, tiled=True)  13.1 us
    pallas_call x1, Pallas kernels, advance(): pl.pallas_call(lambda *refs: advance_body(*refs, levels=levels, cells=cel...  8.38 us
    all_to_all x1, starting transfers between devices, shards(): held = lax.all_to_all(send, 'tile', 0, 0, tiled=True)  7.41 us
    all_to_all x1, waiting for transfers between devices, shards(): held = lax.all_to_all(send, 'tile', 0, 0, tiled=True)  6.45 us
    pallas_call x1, Pallas kernels, pack(): pl.pallas_call(lambda a, o: pack_body(a, o, levels=levels, cells=cells),...  4.86 us
    pallas_call x1, Pallas kernels, route(): pl.pallas_call(route_body, out_shape=jax.ShapeDtypeStruct(rows.shape, row...  2.24 us
  transfers between devices with their start and end apart: 1, of which 1 were waited for; matrix products, arithmetic and copies ran while one was open for 5% of the time, Pallas kernels for 0%

profile of v1, /device:TPU:0, one launch (start us, length us, event | category | flops | bytes accessed | tf_op | source)
XLA Modules:
  0.0 45.7 jit_solution(6058188801602147985)
XLA Ops:
  0.0 0.0 copy-start.1
  0.0 4.9 %pack.1.refs_4_ = f32[16,24,128]{2,1,0:T(8,128)} custom-call(f32[6,8,128,128]{3,2,1,0:T(8,128)} %bitcast.22), custom_call_target="tpu_custom_call" | custom-call | tf_op jit(solution)/shard_map/pack/pallas_call | solution.py:43
  4.9 7.4 %all-to-all-start = ((f32[16,24,128]{2,1,0:T(8,128)}), f32[16,24,128]{2,1,0:T(8,128)S(1)}, u32[]{:S(2)}, u32[]{:S(2)}) async-start(f32[16,24,128]{2,1,0:T(8,128)} %pack.1.refs_4_), calls=%async_computation | async-start | bytes 393216 | tf_op jit(solution)/shard_map/all_to_all | solution.py:231
  12.4 0.0 copy-done.1
  12.4 0.1 copy.7
  12.5 0.1 reshape.227
  12.6 0.1 broadcast_in_dim.109
  12.7 0.1 broadcast_in_dim.103
  12.8 0.1 broadcast_in_dim.101
  13.0 0.1 broadcast_in_dim.99
  13.1 0.1 add.245
  13.2 0.1 sub.75
  13.3 0.1 add.237
  13.4 0.1 add.240
  13.5 0.1 broadcast_in_dim.113
  13.6 0.1 broadcast_in_dim.107
  13.7 0.1 broadcast_in_dim.105
  13.8 0.1 broadcast_in_dim.111
  13.9 0.1 add.226
  14.0 0.1 add.233
  14.1 0.1 add.230
  14.2 0.6 %fusion.6.index_ref = s32[3,128]{1,0:T(4,128)} fusion(s32[3,128]{1,0:T(4,128)S(1)} %add.233, s32[3,128]{1,0:T(4,128)S(1)} %add.230, s32[3,128]{1,0:T(4,128)S(1)} %add.245, s32[3,128]{1,0:T(4,128)S(1)} %add.240, pred[3,128]{1,0:T(4,128)(4,1)S(1)} %broadcast_in_dim.107, s32[3,128]{1,0:T(4,128)S(1)} %add.237, s32[3,128]{1,0:T(4,128)S(1)} %add.226, ...), kind=kLoop, calls=%fused_computation.31 | loop fusion | flops 30336 | bytes 15360 | tf_op jit(solution)/shard_map/add | solution.py:217
  14.8 6.4 %all-to-all-done = f32[16,24,128]{2,1,0:T(8,128)S(1)} async-done(((f32[16,24,128]{2,1,0:T(8,128)}), f32[16,24,128]{2,1,0:T(8,128)S(1)}, u32[]{:S(2)}, u32[]{:S(2)}) %all-to-all-start) | async-done | bytes 196640 | tf_op jit(solution)/shard_map/all_to_all | solution.py:231
  21.2 0.0 copy-start
  21.3 0.7 %copy-done = f32[16,24,128]{2,1,0:T(8,128)} copy-done((f32[16,24,128]{2,1,0:T(8,128)}, f32[16,24,128]{2,1,0:T(8,128)S(1)}, u32[]{:S(2)}) %copy-start) | copy-done | bytes 196632
  21.9 2.2 %route.1 = f32[384,128]{1,0:T(8,128)} custom-call(s32[3,128]{1,0:T(4,128)} %fusion.6.index_ref, f32[384,128]{1,0:T(8,128)} %bitcast.27), custom_call_target="tpu_custom_call" | custom-call | tf_op jit(solution)/shard_map/route/pallas_call | solution.py:79
  24.2 13.1 %all_to_all.10.refs_5_ = f32[16,24,128]{2,1,0:T(8,128)} all-to-all(f32[16,24,128]{2,1,0:T(8,128)} %bitcast.28), channel_id=1, replica_groups=mesh['groups'=2,'tile'=16] {'tile'}, dimensions={0} | all-to-all | bytes 393216 | tf_op jit(solution)/shard_map/all_to_all | solution.py:234
  37.3 8.4 %advance.1 = f32[6,8,128,128]{3,2,1,0:T(8,128)} custom-call(f32[6,8,128,128]{3,2,1,0:T(8,128)} %bitcast.23, bf16[6,8,128,128]{3,2,1,0:T(8,128)(2,1)} %bitcast.24, bf16[6,8,128,128]{3,2,1,0:T(8,128)(2,1)} %bitcast.25, bf16[6,8,128,128]{3,2,1,0:T(8,128)(2,1)} %bitcast.26, f32[16,24,128]{2,1,0:T(8,128)} %pack.1.refs_4_, f32[16,24,128]{2,1,0:T(8,128)} %all_to_all.10.refs_5_), custom_call_target="tpu_custom_call" | custom-call | tf_op jit(solution)/shard_map/advance/pallas_call | solution.py:170
  (27 shorter events, 0.2 us)
Async XLA Ops:
  0.0 12.4 %copy-start.1 = (s32[6,4,3]{0,1,2:T(4,128)S(1)}, s32[6,4,3]{0,1,2:T(4,128)}, u32[]{:S(2)}) copy-start(s32[6,4,3]{0,1,2:T(4,128)} %param.9) | copy-start | bytes 868
  4.9 16.4 %all-to-all-start = ((f32[16,24,128]{2,1,0:T(8,128)}), f32[16,24,128]{2,1,0:T(8,128)S(1)}, u32[]{:S(2)}, u32[]{:S(2)}) async-start(f32[16,24,128]{2,1,0:T(8,128)} %pack.1.refs_4_), calls=%async_computation | async-start | bytes 393216 | tf_op jit(solution)/shard_map/all_to_all | solution.py:231
  21.2 0.7 %copy-start = (f32[16,24,128]{2,1,0:T(8,128)}, f32[16,24,128]{2,1,0:T(8,128)S(1)}, u32[]{:S(2)}) copy-start(f32[16,24,128]{2,1,0:T(8,128)S(1)} %all-to-all-done) | copy-start | bytes 589828

commit v2 on v1

v2 whole, which is shorter than its diff:
```python
import math

import jax
import jax.numpy as jnp
from jax import lax
from jax.experimental import pallas as pl
from jax.experimental.pallas import tpu as pltpu
from jax.sharding import PartitionSpec as P

DEPTH = 2
EARLY = 3


def split3(x):
    hi = x.astype(jnp.bfloat16)
    rest = x - hi.astype(jnp.float32)
    mid = rest.astype(jnp.bfloat16)
    low = (rest - mid.astype(jnp.float32)).astype(jnp.bfloat16)
    return hi, mid, low


def pack_body(tracer_ref, out_ref, *, count, levels, cells):
    lane = lax.broadcasted_iota(jnp.int32, (cells, cells), 1)
    group = lane // (2 * DEPTH)
    for p in range(count):
        packed = jnp.zeros((cells, cells), jnp.float32)
        for k in range(levels):
            turned = pltpu.roll(tracer_ref[p, k], 2 * DEPTH * k + DEPTH, 1)
            packed = jnp.where(group == k, turned, packed)
        rows = packed.T
        for k in range(levels):
            for d in range(DEPTH):
                m = d * levels + k
                south = 2 * DEPTH * k + DEPTH + d
                north = 2 * DEPTH * k + DEPTH - 1 - d
                slot = p * 4
                out_ref[m, slot : slot + 1, :] = rows[south : south + 1]
                out_ref[m, slot + 1 : slot + 2, :] = tracer_ref[p, k, cells - 1 - d : cells - d, :]
                out_ref[m, slot + 2 : slot + 3, :] = rows[north : north + 1]
                out_ref[m, slot + 3 : slot + 4, :] = tracer_ref[p, k, d : d + 1, :]


def pack(panels):
    total, levels, cells, _ = panels.shape
    count = 2
    return pl.pallas_call(
        lambda a, o: pack_body(a, o, count=count, levels=levels, cells=cells),
        grid=(total // count,),
        in_specs=[pl.BlockSpec((count, levels, cells, cells), lambda p: (p, 0, 0, 0))],
        out_specs=pl.BlockSpec((levels * DEPTH, count * 4, cells), lambda p: (0, p, 0)),
        out_shape=jax.ShapeDtypeStruct((levels * DEPTH, total * 4, cells), jnp.float32),
        name="pack",
    )(panels)


def route_body(index_ref, rows_ref, out_ref):
    total, cells = rows_ref.shape
    source = lax.broadcasted_iota(jnp.int32, (cells, cells), 0)
    target = lax.broadcasted_iota(jnp.int32, (cells, cells), 1)
    flip = (source + target == cells - 1).astype(jnp.float32).astype(jnp.bfloat16)
    parts = split3(rows_ref[...])
    flipped = [
        jnp.dot(part, flip, preferred_element_type=jnp.float32).astype(jnp.bfloat16)
        for part in parts
    ]
    both = jnp.concatenate(
        [jnp.concatenate(parts, axis=1), jnp.concatenate(flipped, axis=1)], axis=0
    )
    numbers = lax.broadcasted_iota(jnp.int32, (2 * total, index_ref.shape[1]), 0)
    width = index_ref.shape[1]
    for c in range(index_ref.shape[0]):
        chosen = (numbers == index_ref[c : c + 1, :]).astype(jnp.float32).astype(jnp.bfloat16)
        got = lax.dot_general(
            chosen, both, (((0,), (0,)), ((), ())), preferred_element_type=jnp.float32
        )
        out_ref[c * width : (c + 1) * width, :] = (
            got[:, :cells] + got[:, cells : 2 * cells]
        ) + got[:, 2 * cells :]


def route(index, rows):
    return pl.pallas_call(
        route_body,
        out_shape=jax.ShapeDtypeStruct(rows.shape, rows.dtype),
        name="route",
    )(index, rows)


def edge_column(line, cells):
    return jnp.where(line < DEPTH, line, cells - 2 * DEPTH + line)


def inner_body(
    tracer_ref, east_ref, north_ref, diff_ref, *refs, levels, cells, step
):
    out_ref, lines_ref, ext_ref, select_ref = refs[-4:]
    lines = 4 * DEPTH

    @pl.when(pl.program_id(0) == 0)
    def _():
        row = lax.broadcasted_iota(jnp.int32, (cells, cells), 0)
        lane = lax.broadcasted_iota(jnp.int32, (cells, cells), 1)
        line = lane % lines
        hit = (row == edge_column(line, cells)) & (line < 2 * DEPTH)
        for n in range(2 * levels):
            select_ref[n] = jnp.where(hit & (lane // lines == n), 1.0, 0.0).astype(jnp.bfloat16)

    columns = jnp.zeros((cells, cells), jnp.float32)
    for k in range(levels):
        columns += jnp.dot(north_ref[0, k], select_ref[k], preferred_element_type=jnp.float32)
        columns += jnp.dot(
            diff_ref[0, k], select_ref[levels + k], preferred_element_type=jnp.float32
        )
    columns = columns.T
    for f, field_ref in ((0, east_ref), (1, diff_ref)):
        for k in range(levels):
            base = (f * levels + k) * lines
            lines_ref[0, f, k, 0 : 2 * DEPTH, :] = columns[base : base + 2 * DEPTH]
            first = field_ref[0, k, 0:16, :].astype(jnp.float32)
            last = field_ref[0, k, cells - 16 : cells, :].astype(jnp.float32)
            lines_ref[0, f, k, 2 * DEPTH : 3 * DEPTH, :] = first[0:DEPTH]
            lines_ref[0, f, k, 3 * DEPTH : 4 * DEPTH, :] = last[16 - DEPTH :]

    for k in range(levels):
        ext_ref[k, 8 : 8 + cells, :] = tracer_ref[0, k]
        ext_ref[k, 0:8, :] = tracer_ref[0, k, cells - 8 : cells, :]
        ext_ref[k, 8 + cells : 16 + cells, :] = tracer_ref[0, k, 0:8, :]

    for start in range(0, cells, step):
        ratios = []
        partial_values = []
        below = None
        for k in range(levels):

            def shifted(offset):
                return ext_ref[k, 8 + start + offset : 8 + start + offset + step, :]

            q = tracer_ref[0, k, start : start + step, :]
            along_first = 8.0 * (shifted(1) - shifted(-1)) - (shifted(2) - shifted(-2))
            along_second = 8.0 * (pltpu.roll(q, cells - 1, 1) - pltpu.roll(q, 1, 1)) - (
                pltpu.roll(q, cells - 2, 1) - pltpu.roll(q, 2, 1)
            )
            east = east_ref[0, k, start : start + step, :].astype(jnp.float32)
            north = north_ref[0, k, start : start + step, :].astype(jnp.float32)
            forced = q - (east * along_first + north * along_second) * (1.0 / 12.0)
            coupling = diff_ref[0, k, start : start + step, :].astype(jnp.float32)
            pivot = 1.0 + coupling
            if k > 0:
                pivot = pivot + below - below * ratios[-1]
                forced = forced + below * partial_values[-1]
            inverse = 1.0 / pivot
            ratios.append(coupling * inverse)
            partial_values.append(forced * inverse)
            below = coupling
        value = partial_values[-1]
        out_ref[0, levels - 1, start : start + step, :] = value
        for k in range(levels - 2, -1, -1):
            value = partial_values[k] + ratios[k] * value
            out_ref[0, k, start : start + step, :] = value


def inner(panels, east, north, diff, first, count, earlier=()):
    total, levels, cells, _ = panels.shape
    lines_shape = (total, 2, levels, 4 * DEPTH, cells)
    block = pl.BlockSpec((1, levels, cells, cells), lambda p: (p + first, 0, 0, 0))
    lines_block = pl.BlockSpec((1,) + lines_shape[1:], lambda p: (p + first, 0, 0, 0, 0))
    return pl.pallas_call(
        lambda *refs: inner_body(*refs, levels=levels, cells=cells, step=16),
        grid=(count,),
        in_specs=[block] * 4 + [pl.BlockSpec(memory_space=pl.ANY)] * len(earlier),
        out_specs=(block, lines_block),
        out_shape=(
            jax.ShapeDtypeStruct(panels.shape, panels.dtype),
            jax.ShapeDtypeStruct(lines_shape, jnp.float32),
        ),
        scratch_shapes=[
            pltpu.VMEM((levels, cells + 16, cells), jnp.float32),
            pltpu.VMEM((2 * levels, cells, cells), jnp.bfloat16),
        ],
        input_output_aliases={4 + n: n for n in range(len(earlier))},
        name="inner",
    )(panels, east, north, diff, *earlier)


def edges_body(
    inner_ref, lines_ref, own_ref, ghost_ref, out_ref, source_ref, spread_ref, *, levels, cells
):
    panel = pl.program_id(0)
    lines = 4 * DEPTH
    depth_rows = levels * lines

    @pl.when(panel == 0)
    def _():
        row = lax.broadcasted_iota(jnp.int32, (depth_rows, cells), 0)
        lane = lax.broadcasted_iota(jnp.int32, (depth_rows, cells), 1)
        line = row % lines
        hit = (lane == edge_column(line, cells)) & (line < 2 * DEPTH)
        for k in range(levels):
            mine = jnp.where(hit & (row // lines == k), 1.0, 0.0).astype(jnp.bfloat16)
            for s in range(3):
                spread_ref[
                    s * depth_rows : (s + 1) * depth_rows, k * cells : (k + 1) * cells
                ] = mine

    def strip(ref, edge, d):
        return ref[d * levels : (d + 1) * levels, pl.ds(panel * 4 + edge, 1), :].reshape(
            levels, cells
        )

    for base, low, high in ((0, 0, 2), (2 * DEPTH, 3, 1)):
        low_0 = strip(ghost_ref, low, 0) - strip(own_ref, high, 0)
        low_1 = strip(ghost_ref, low, 1) - strip(own_ref, high, 1)
        high_0 = strip(ghost_ref, high, 0) - strip(own_ref, low, 0)
        high_1 = strip(ghost_ref, high, 1) - strip(own_ref, low, 1)
        source_ref[:, base, :] = low_1 - 8.0 * low_0
        source_ref[:, base + 1, :] = low_0
        source_ref[:, base + 2, :] = -high_0
        source_ref[:, base + 3, :] = 8.0 * high_0 - high_1

    ratios = []
    partial_values = []
    below = None
    for k in range(levels):
        forced = lines_ref[0, 0, k] * source_ref[k] * (-1.0 / 12.0)
        coupling = lines_ref[0, 1, k]
        pivot = 1.0 + coupling
        if k > 0:
            pivot = pivot + below - below * ratios[-1]
            forced = forced + below * partial_values[-1]
        inverse = 1.0 / pivot
        ratios.append(coupling * inverse)
        partial_values.append(forced * inverse)
        below = coupling
    solved = [partial_values[-1]]
    for k in range(levels - 2, -1, -1):
        solved.insert(0, partial_values[k] + ratios[k] * solved[0])

    parts = split3(jnp.concatenate(solved, axis=0))
    stacked = jnp.concatenate([part.astype(jnp.float32) for part in parts], axis=0)
    added = jnp.dot(
        stacked.T.astype(jnp.bfloat16), spread_ref[...], preferred_element_type=jnp.float32
    )
    for k in range(levels):
        value = inner_ref[0, k] + added[:, k * cells : (k + 1) * cells]
        out_ref[0, k] = value
        out_ref[0, k, 0:DEPTH, :] = value[0:DEPTH] + solved[k][2 * DEPTH : 3 * DEPTH]
        out_ref[0, k, cells - DEPTH : cells, :] = (
            value[cells - DEPTH :] + solved[k][3 * DEPTH :]
        )


def edges(inner_values, lines, own, ghosts):
    count, levels, cells, _ = inner_values.shape
    block = pl.BlockSpec((1, levels, cells, cells), lambda p: (p, 0, 0, 0))
    rows = levels * DEPTH
    strips = pl.BlockSpec((rows,) + own.shape[1:], lambda p: (0, 0, 0))
    depth_rows = levels * 4 * DEPTH
    return pl.pallas_call(
        lambda *refs: edges_body(*refs, levels=levels, cells=cells),
        grid=(count,),
        in_specs=[
            block,
            pl.BlockSpec((1,) + lines.shape[1:], lambda p: (p, 0, 0, 0, 0)),
            strips,
            strips,
        ],
        out_specs=block,
        out_shape=jax.ShapeDtypeStruct(inner_values.shape, inner_values.dtype),
        scratch_shapes=[
            pltpu.VMEM((levels, 4 * DEPTH, cells), jnp.float32),
            pltpu.VMEM((3 * depth_rows, levels * cells), jnp.bfloat16),
        ],
        input_output_aliases={0: 0},
        name="edges",
    )(inner_values, lines, own, ghosts)


def row_sources(seam_table, across, cells):
    total = across * across
    flat = seam_table.reshape(24, 3)
    codes = jnp.tile((flat[:, 0] * 4 + flat[:, 1]) * 2 + flat[:, 2], total).reshape(-1, cells)
    number = lax.broadcasted_iota(jnp.int32, codes.shape, 0) * cells + lax.broadcasted_iota(
        jnp.int32, codes.shape, 1
    )
    device = number // 24
    slot = number % 24
    panel = slot // 4
    edge = slot % 4
    far_panel = codes // 8
    far_edge = codes // 2 % 4
    turned = codes % 2 == 1
    shift = total // 2 + 1
    tile = (device - panel % 2 * shift) % total
    row = tile // across
    col = tile % across
    last = across - 1
    on_edge = jnp.where(
        edge == 0, col == 0, jnp.where(edge == 1, row == last, jnp.where(edge == 2, col == last, row == 0))
    )
    along = jnp.where(edge % 2 == 0, row, col)
    spot = jnp.where(turned, last - along, along)
    far_tile = jnp.where(
        far_edge == 0,
        spot * across,
        jnp.where(far_edge == 1, last * across + spot, jnp.where(far_edge == 2, spot * across + last, spot)),
    )
    far_device = (far_tile + far_panel % 2 * shift) % total
    step = jnp.where(edge == 0, -1, jnp.where(edge == 1, across, jnp.where(edge == 2, 1, -across)))
    near_device = (device + step) % total
    source = jnp.where(
        on_edge,
        far_device * 24 + far_panel * 4 + far_edge,
        near_device * 24 + panel * 4 + (edge + 2) % 4,
    )
    return source + jnp.where(on_edge & turned, total * 24, 0)


def shards(tracer, courant_east, courant_north, diffusivity, seam_table):
    panels = tracer[0]
    fields = (panels, courant_east[0], courant_north[0], diffusivity[0])
    tile_count = lax.axis_size("tile")
    across = math.isqrt(tile_count)
    cells = panels.shape[-1]
    own = pack(panels)
    rows = own.shape[0]
    assert tile_count >= rows
    send = own
    if tile_count > rows:
        send = jnp.pad(own, ((0, tile_count - rows), (0, 0), (0, 0)))
    held = lax.all_to_all(send, "tile", 0, 0, tiled=True)
    early = EARLY
    begun = inner(*fields, 0, early)
    index = row_sources(seam_table, across, cells)
    held, index, begun = lax.optimization_barrier((held, index, begun))
    routed = route(index, held.reshape(-1, cells))
    ghosts = lax.all_to_all(routed.reshape(held.shape), "tile", 0, 0, tiled=True)
    whole = inner(*fields, early, panels.shape[0] - early, begun)
    return edges(*whole, own, ghosts)[None]


def solution(mesh):
    placed = P(("groups", "tile"), None, None, None, None)
    return jax.shard_map(
        shards,
        mesh=mesh,
        in_specs=(placed, placed, placed, placed, P()),
        out_specs=placed,
        check_vma=False,
    )
```

time: 46.2 us -> 43.4 us (0.939)
  blocking collectives: 13.1 us -> 0 us
  Pallas kernels: 15.5 us -> 22.7 us
  starting transfers between devices: 7.41 us -> 10.9 us
  local copies, waits for them, and re-layouts: 2.27 us -> 1.65 us
    all_to_all x1 -> x0, blocking collectives: 13.1 us -> none  [shards(): lax.all_to_all(routed.reshape(held.shape), 'tile', 0, 0, tiled=True)]
    pallas_call x2 -> x4, Pallas kernels: 13.2 us -> 20.5 us  [the longest x2 10.2 us: inner(): pl.pallas_call(lambda *refs: inner_body(*refs, levels=levels, cells=cells...]
    all_to_all x0 -> x1, waiting for transfers between devices: none -> 3.84 us  [shards(): lax.all_to_all(routed.reshape(held.shape), 'tile', 0, 0, tiled=True)]
    all_to_all x1, waiting for transfers between devices: 6.45 us -> 2.84 us  [shards(): held = lax.all_to_all(send, 'tile', 0, 0, tiled=True)]
    all_to_all x0 -> x1, starting transfers between devices: none -> 3.52 us  [shards(): lax.all_to_all(routed.reshape(held.shape), 'tile', 0, 0, tiled=True)]
    broadcast_in_dim x16 -> x0, local copies, waits for them, and re-layouts: 0.8 us -> none  [the longest x2 0.1 us: row_sources(): jnp.where(far_edge == 2, spot * across + last, spot)]
    unnamed x5 -> x7, local copies, waits for them, and re-layouts: 0.79 us -> 1.47 us
    add x11 -> x0, local copies, waits for them, and re-layouts: 0.52 us -> none  [the longest x4 0.17 us: row_sources(): near_device * 24 + panel * 4 + (edge + 2) % 4]
  transfers between devices with their start and end apart: 1 -> 2, of which waited for: 1 -> 2; matrix products, arithmetic and copies ran while one was open for 5% -> 2% of each run, Pallas kernels for 0% -> 24%
where the time goes in v2:
time: 43.4 us; the launch traced here: 42.8 us
  Pallas kernels  22.7 us (52%)
  starting transfers between devices  10.9 us (25%)
  waiting for transfers between devices  6.69 us (15%)
  local copies, waits for them, and re-layouts  1.65 us (4%)
  other arithmetic  0.74 us (2%)
    pallas_call x2, Pallas kernels, inner(): pl.pallas_call(lambda *refs: inner_body(*refs, levels=levels, cells=cells...  10.2 us
    all_to_all x1, starting transfers between devices, shards(): held = lax.all_to_all(send, 'tile', 0, 0, tiled=True)  7.41 us
    pallas_call x1, Pallas kernels, edges(): pl.pallas_call(lambda *refs: edges_body(*refs, levels=levels, cells=cells...  6.36 us
    pallas_call x1, Pallas kernels, pack(): pl.pallas_call(lambda a, o: pack_body(a, o, count=count, levels=levels, c...  3.95 us
    all_to_all x1, waiting for transfers between devices, shards(): lax.all_to_all(routed.reshape(held.shape), 'tile', 0, 0, tiled=True)  3.84 us
    all_to_all x1, starting transfers between devices, shards(): lax.all_to_all(routed.reshape(held.shape), 'tile', 0, 0, tiled=True)  3.52 us
    all_to_all x1, waiting for transfers between devices, shards(): held = lax.all_to_all(send, 'tile', 0, 0, tiled=True)  2.84 us
    pallas_call x1, Pallas kernels, route(): pl.pallas_call(route_body, out_shape=jax.ShapeDtypeStruct(rows.shape, row...  2.24 us
  transfers between devices with their start and end apart: 2, of which 2 were waited for; matrix products, arithmetic and copies ran while one was open for 2% of the time, Pallas kernels for 24%

profile of v2, /device:TPU:0, one launch (start us, length us, event | category | flops | bytes accessed | tf_op | source)
XLA Modules:
  0.0 42.8 jit_solution(6760837849570907220)
XLA Ops:
  0.0 0.0 copy-start.2
  0.0 4.0 %pack.1.refs_2_ = f32[16,24,128]{2,1,0:T(8,128)} custom-call(f32[6,8,128,128]{3,2,1,0:T(8,128)} %bitcast.11), custom_call_target="tpu_custom_call" | custom-call | tf_op jit(solution)/shard_map/pack/pallas_call | solution.py:46
  4.0 7.4 %all-to-all-start = ((f32[16,24,128]{2,1,0:T(8,128)}), f32[16,24,128]{2,1,0:T(8,128)S(1)}, u32[]{:S(2)}, u32[]{:S(2)}) async-start(f32[16,24,128]{2,1,0:T(8,128)} %pack.1.refs_2_), calls=%async_computation | async-start | bytes 393216 | tf_op jit(solution)/shard_map/all_to_all | solution.py:330
  11.4 0.0 copy-done.2
  11.4 0.1 copy.10
  11.5 0.1 reshape.31
  11.6 0.1 reshape_tile.3
  11.7 5.1 %inner.2 = (f32[6,8,128,128]{3,2,1,0:T(8,128)}, f32[6,2,8,8,128]{4,3,2,1,0:T(8,128)}) custom-call(f32[6,8,128,128]{3,2,1,0:T(8,128)} %bitcast.12, bf16[6,8,128,128]{3,2,1,0:T(8,128)(2,1)} %bitcast.14, bf16[6,8,128,128]{3,2,1,0:T(8,128)(2,1)} %bitcast.16, bf16[6,8,128,128]{3,2,1,0:T(8,128)(2,1)} %bitcast.18), custom_call_target="tpu_custom_call" | custom-call | tf_op jit(solution)/shard_map/inner/pallas_call | solution.py:167
  16.8 0.7 %fusion.17.index_ref = s32[3,128]{1,0:T(4,128)} fusion(s32[3,128]{1,0:T(4,128)S(1)} %reshape_tile.3, s32[3]{0:T(128)S(1)} %iota_multiply_fusion), kind=kLoop, calls=%fused_computation.62 | loop fusion | flops 81792 | bytes 3084 | tf_op jit(solution)/shard_map/add | solution.py:315
  17.5 2.8 %all-to-all-done = f32[16,24,128]{2,1,0:T(8,128)S(1)} async-done(((f32[16,24,128]{2,1,0:T(8,128)}), f32[16,24,128]{2,1,0:T(8,128)S(1)}, u32[]{:S(2)}, u32[]{:S(2)}) %all-to-all-start) | async-done | bytes 196640 | tf_op jit(solution)/shard_map/all_to_all | solution.py:330
  20.3 0.0 copy-start.1
  20.3 0.7 %copy-done.1 = f32[16,24,128]{2,1,0:T(8,128)} copy-done((f32[16,24,128]{2,1,0:T(8,128)}, f32[16,24,128]{2,1,0:T(8,128)S(1)}, u32[]{:S(2)}) %copy-start.1) | copy-done | bytes 196632
  21.0 2.2 %route.1 = f32[384,128]{1,0:T(8,128)} custom-call(s32[3,128]{1,0:T(4,128)} %fusion.17.index_ref, f32[384,128]{1,0:T(8,128)} %bitcast.20), custom_call_target="tpu_custom_call" | custom-call | tf_op jit(solution)/shard_map/route/pallas_call | solution.py:82
  23.3 3.5 %all-to-all-start.1 = ((f32[16,24,128]{2,1,0:T(8,128)}), f32[16,24,128]{2,1,0:T(8,128)S(1)}, u32[]{:S(2)}, u32[]{:S(2)}) async-start(f32[16,24,128]{2,1,0:T(8,128)} %bitcast.21), calls=%async_computation.1 | async-start | bytes 393216 | tf_op jit(solution)/shard_map/all_to_all | solution.py:336
  26.8 5.1 %inner.3 = (f32[6,8,128,128]{3,2,1,0:T(8,128)}, f32[6,2,8,8,128]{4,3,2,1,0:T(8,128)}) custom-call(f32[6,8,128,128]{3,2,1,0:T(8,128)} %bitcast.13, bf16[6,8,128,128]{3,2,1,0:T(8,128)(2,1)} %bitcast.15, bf16[6,8,128,128]{3,2,1,0:T(8,128)(2,1)} %bitcast.17, bf16[6,8,128,128]{3,2,1,0:T(8,128)(2,1)} %bitcast.19, ...), custom_call_target="tpu_custom_call", output_to_operand_aliasing={{0}: (4, {}), {1}: (5, {})} | custom-call | tf_op jit(solution)/shard_map/inner/pallas_call | solution.py:167
  31.9 3.8 %all-to-all-done.1.refs_3_ = f32[16,24,128]{2,1,0:T(8,128)S(1)} async-done(((f32[16,24,128]{2,1,0:T(8,128)}), f32[16,24,128]{2,1,0:T(8,128)S(1)}, u32[]{:S(2)}, u32[]{:S(2)}) %all-to-all-start.1) | async-done | bytes 196640 | tf_op jit(solution)/shard_map/all_to_all | solution.py:336
  35.7 0.0 copy-start
  35.7 0.7 %copy-done = f32[16,24,128]{2,1,0:T(8,128)} copy-done((f32[16,24,128]{2,1,0:T(8,128)}, f32[16,24,128]{2,1,0:T(8,128)S(1)}, u32[]{:S(2)}) %copy-start) | copy-done | bytes 196632
  36.4 6.4 %edges.1 = f32[6,8,128,128]{3,2,1,0:T(8,128)} custom-call(f32[6,8,128,128]{3,2,1,0:T(8,128)} %get-tuple-element.17.refs_0_, f32[6,2,8,8,128]{4,3,2,1,0:T(8,128)} %get-tuple-element.18.refs_1_, f32[16,24,128]{2,1,0:T(8,128)} %pack.1.refs_2_, f32[16,24,128]{2,1,0:T(8,128)} %copy-done), custom_call_target="tpu_custom_call", output_to_operand_aliasing={{}: (0, {})} | custom-call | tf_op jit(solution)/shard_map/edges/pallas_call | solution.py:258
  (3 shorter events, 0.0 us)
Async XLA Ops:
  0.0 11.4 %copy-start.2 = (s32[6,4,3]{0,1,2:T(4,128)S(1)}, s32[6,4,3]{0,1,2:T(4,128)}, u32[]{:S(2)}) copy-start(s32[6,4,3]{0,1,2:T(4,128)} %param.9) | copy-start | bytes 868
  4.0 16.4 %all-to-all-start = ((f32[16,24,128]{2,1,0:T(8,128)}), f32[16,24,128]{2,1,0:T(8,128)S(1)}, u32[]{:S(2)}, u32[]{:S(2)}) async-start(f32[16,24,128]{2,1,0:T(8,128)} %pack.1.refs_2_), calls=%async_computation | async-start | bytes 393216 | tf_op jit(solution)/shard_map/all_to_all | solution.py:330
  20.3 0.7 %copy-start.1 = (f32[16,24,128]{2,1,0:T(8,128)}, f32[16,24,128]{2,1,0:T(8,128)S(1)}, u32[]{:S(2)}) copy-start(f32[16,24,128]{2,1,0:T(8,128)S(1)} %all-to-all-done) | copy-start | bytes 589828
  23.3 12.5 %all-to-all-start.1 = ((f32[16,24,128]{2,1,0:T(8,128)}), f32[16,24,128]{2,1,0:T(8,128)S(1)}, u32[]{:S(2)}, u32[]{:S(2)}) async-start(f32[16,24,128]{2,1,0:T(8,128)} %bitcast.21), calls=%async_computation.1 | async-start | bytes 393216 | tf_op jit(solution)/shard_map/all_to_all | solution.py:336
  35.7 0.7 %copy-start = (f32[16,24,128]{2,1,0:T(8,128)}, f32[16,24,128]{2,1,0:T(8,128)S(1)}, u32[]{:S(2)}) copy-start(f32[16,24,128]{2,1,0:T(8,128)S(1)} %all-to-all-done.1.refs_3_) | copy-start | bytes 589828

commit v3 on v2

--- a/solution.py
+++ b/solution.py
@@ -66,13 +66,14 @@
     both = jnp.concatenate(
         [jnp.concatenate(parts, axis=1), jnp.concatenate(flipped, axis=1)], axis=0
     )
-    numbers = lax.broadcasted_iota(jnp.int32, (2 * total, index_ref.shape[1]), 0)
     width = index_ref.shape[1]
+    numbers = lax.broadcasted_iota(jnp.int32, (width, 2 * total), 1).astype(jnp.float32)
+    wanted = index_ref[...].astype(jnp.float32)
     for c in range(index_ref.shape[0]):
-        chosen = (numbers == index_ref[c : c + 1, :]).astype(jnp.float32).astype(jnp.bfloat16)
-        got = lax.dot_general(
-            chosen, both, (((0,), (0,)), ((), ())), preferred_element_type=jnp.float32
-        )
+        spread = jnp.broadcast_to(wanted[c : c + 1, :], (width, width)).T
+        spread = jnp.concatenate([spread] * (2 * total // width), axis=1)
+        chosen = jnp.where(spread == numbers, 1.0, 0.0).astype(jnp.bfloat16)
+        got = jnp.dot(chosen, both, preferred_element_type=jnp.float32)
         out_ref[c * width : (c + 1) * width, :] = (
             got[:, :cells] + got[:, cells : 2 * cells]
         ) + got[:, 2 * cells :]
@@ -87,7 +88,7 @@
 
 
 def edge_column(line, cells):
-    return jnp.where(line < DEPTH, line, cells - 2 * DEPTH + line)
+    return (cells - DEPTH + line) % cells
 
 
 def inner_body(
@@ -118,8 +119,8 @@
             lines_ref[0, f, k, 0 : 2 * DEPTH, :] = columns[base : base + 2 * DEPTH]
             first = field_ref[0, k, 0:16, :].astype(jnp.float32)
             last = field_ref[0, k, cells - 16 : cells, :].astype(jnp.float32)
-            lines_ref[0, f, k, 2 * DEPTH : 3 * DEPTH, :] = first[0:DEPTH]
-            lines_ref[0, f, k, 3 * DEPTH : 4 * DEPTH, :] = last[16 - DEPTH :]
+            lines_ref[0, f, k, 2 * DEPTH : 3 * DEPTH, :] = last[16 - DEPTH :]
+            lines_ref[0, f, k, 3 * DEPTH : 4 * DEPTH, :] = first[0:DEPTH]
 
     for k in range(levels):
         ext_ref[k, 8 : 8 + cells, :] = tracer_ref[0, k]
@@ -182,25 +183,9 @@
     )(panels, east, north, diff, *earlier)
 
 
-def edges_body(
-    inner_ref, lines_ref, own_ref, ghost_ref, out_ref, source_ref, spread_ref, *, levels, cells
-):
+def edges_body(inner_ref, lines_ref, own_ref, ghost_ref, out_ref, source_ref, *, levels, cells):
     panel = pl.program_id(0)
     lines = 4 * DEPTH
-    depth_rows = levels * lines
-
-    @pl.when(panel == 0)
-    def _():
-        row = lax.broadcasted_iota(jnp.int32, (depth_rows, cells), 0)
-        lane = lax.broadcasted_iota(jnp.int32, (depth_rows, cells), 1)
-        line = row % lines
-        hit = (lane == edge_column(line, cells)) & (line < 2 * DEPTH)
-        for k in range(levels):
-            mine = jnp.where(hit & (row // lines == k), 1.0, 0.0).astype(jnp.bfloat16)
-            for s in range(3):
-                spread_ref[
-                    s * depth_rows : (s + 1) * depth_rows, k * cells : (k + 1) * cells
-                ] = mine
 
     def strip(ref, edge, d):
         return ref[d * levels : (d + 1) * levels, pl.ds(panel * 4 + edge, 1), :].reshape(
@@ -212,10 +197,10 @@
         low_1 = strip(ghost_ref, low, 1) - strip(own_ref, high, 1)
         high_0 = strip(ghost_ref, high, 0) - strip(own_ref, low, 0)
         high_1 = strip(ghost_ref, high, 1) - strip(own_ref, low, 1)
-        source_ref[:, base, :] = low_1 - 8.0 * low_0
-        source_ref[:, base + 1, :] = low_0
-        source_ref[:, base + 2, :] = -high_0
-        source_ref[:, base + 3, :] = 8.0 * high_0 - high_1
+        source_ref[:, base, :] = -high_0
+        source_ref[:, base + 1, :] = 8.0 * high_0 - high_1
+        source_ref[:, base + 2, :] = low_1 - 8.0 * low_0
+        source_ref[:, base + 3, :] = low_0
 
     ratios = []
     partial_values = []
@@ -235,17 +220,17 @@
     for k in range(levels - 2, -1, -1):
         solved.insert(0, partial_values[k] + ratios[k] * solved[0])
 
-    parts = split3(jnp.concatenate(solved, axis=0))
-    stacked = jnp.concatenate([part.astype(jnp.float32) for part in parts], axis=0)
-    added = jnp.dot(
-        stacked.T.astype(jnp.bfloat16), spread_ref[...], preferred_element_type=jnp.float32
-    )
+    blank = jnp.zeros((cells - levels * lines, cells), jnp.float32)
+    columns = jnp.concatenate(solved + [blank], axis=0).T
+    lane = lax.broadcasted_iota(jnp.int32, (cells, cells), 1)
+    outer = (lane < DEPTH) | (lane >= cells - DEPTH)
     for k in range(levels):
-        value = inner_ref[0, k] + added[:, k * cells : (k + 1) * cells]
+        moved = pltpu.roll(columns, (cells - DEPTH - k * lines) % cells, 1)
+        value = inner_ref[0, k] + jnp.where(outer, moved, 0.0)
         out_ref[0, k] = value
-        out_ref[0, k, 0:DEPTH, :] = value[0:DEPTH] + solved[k][2 * DEPTH : 3 * DEPTH]
+        out_ref[0, k, 0:DEPTH, :] = value[0:DEPTH] + solved[k][3 * DEPTH :]
         out_ref[0, k, cells - DEPTH : cells, :] = (
-            value[cells - DEPTH :] + solved[k][3 * DEPTH :]
+            value[cells - DEPTH :] + solved[k][2 * DEPTH : 3 * DEPTH]
         )
 
 
@@ -254,7 +239,6 @@
     block = pl.BlockSpec((1, levels, cells, cells), lambda p: (p, 0, 0, 0))
     rows = levels * DEPTH
     strips = pl.BlockSpec((rows,) + own.shape[1:], lambda p: (0, 0, 0))
-    depth_rows = levels * 4 * DEPTH
     return pl.pallas_call(
         lambda *refs: edges_body(*refs, levels=levels, cells=cells),
         grid=(count,),
@@ -268,7 +252,6 @@
         out_shape=jax.ShapeDtypeStruct(inner_values.shape, inner_values.dtype),
         scratch_shapes=[
             pltpu.VMEM((levels, 4 * DEPTH, cells), jnp.float32),
-            pltpu.VMEM((3 * depth_rows, levels * cells), jnp.bfloat16),
         ],
         input_output_aliases={0: 0},
         name="edges",

time: 43.4 us -> 43.5 us (level)
  no operation moved by 1% of the time
where the time goes in v3:
time: 43.5 us; the launch traced here: 42.9 us
  Pallas kernels  22.9 us (53%)
  starting transfers between devices  10.9 us (25%)
  waiting for transfers between devices  6.68 us (15%)
  local copies, waits for them, and re-layouts  1.65 us (4%)
  other arithmetic  0.74 us (2%)
    pallas_call x2, Pallas kernels, inner(): pl.pallas_call(lambda *refs: inner_body(*refs, levels=levels, cells=cells...  10.2 us
    all_to_all x1, starting transfers between devices, shards(): held = lax.all_to_all(send, 'tile', 0, 0, tiled=True)  7.41 us
    pallas_call x1, Pallas kernels, edges(): pl.pallas_call(lambda *refs: edges_body(*refs, levels=levels, cells=cells...  6.54 us
    pallas_call x1, Pallas kernels, pack(): pl.pallas_call(lambda a, o: pack_body(a, o, count=count, levels=levels, c...  3.95 us
    all_to_all x1, waiting for transfers between devices, shards(): lax.all_to_all(routed.reshape(held.shape), 'tile', 0, 0, tiled=True)  3.84 us
    all_to_all x1, starting transfers between devices, shards(): lax.all_to_all(routed.reshape(held.shape), 'tile', 0, 0, tiled=True)  3.52 us
    all_to_all x1, waiting for transfers between devices, shards(): held = lax.all_to_all(send, 'tile', 0, 0, tiled=True)  2.84 us
    pallas_call x1, Pallas kernels, route(): pl.pallas_call(route_body, out_shape=jax.ShapeDtypeStruct(rows.shape, row...  2.24 us
  transfers between devices with their start and end apart: 2, of which 2 were waited for; matrix products, arithmetic and copies ran while one was open for 2% of the time, Pallas kernels for 24%

profile of v3, /device:TPU:0, one launch (start us, length us, event | category | flops | bytes accessed | tf_op | source)
XLA Modules:
  0.0 42.9 jit_solution(8252104682807296151)
XLA Ops:
  0.0 0.0 copy-start.2
  0.0 4.0 %pack.1.refs_2_ = f32[16,24,128]{2,1,0:T(8,128)} custom-call(f32[6,8,128,128]{3,2,1,0:T(8,128)} %bitcast.11), custom_call_target="tpu_custom_call" | custom-call | tf_op jit(solution)/shard_map/pack/pallas_call | solution.py:46
  4.0 7.4 %all-to-all-start = ((f32[16,24,128]{2,1,0:T(8,128)}), f32[16,24,128]{2,1,0:T(8,128)S(1)}, u32[]{:S(2)}, u32[]{:S(2)}) async-start(f32[16,24,128]{2,1,0:T(8,128)} %pack.1.refs_2_), calls=%async_computation | async-start | bytes 393216 | tf_op jit(solution)/shard_map/all_to_all | solution.py:313
  11.4 0.0 copy-done.2
  11.4 0.1 copy.10
  11.5 0.1 reshape.31
  11.6 0.1 reshape_tile.3
  11.7 5.1 %inner.2 = (f32[6,8,128,128]{3,2,1,0:T(8,128)}, f32[6,2,8,8,128]{4,3,2,1,0:T(8,128)}) custom-call(f32[6,8,128,128]{3,2,1,0:T(8,128)} %bitcast.12, bf16[6,8,128,128]{3,2,1,0:T(8,128)(2,1)} %bitcast.14, bf16[6,8,128,128]{3,2,1,0:T(8,128)(2,1)} %bitcast.16, bf16[6,8,128,128]{3,2,1,0:T(8,128)(2,1)} %bitcast.18), custom_call_target="tpu_custom_call" | custom-call | tf_op jit(solution)/shard_map/inner/pallas_call | solution.py:168
  16.8 0.7 %fusion.17.index_ref = s32[3,128]{1,0:T(4,128)} fusion(s32[3,128]{1,0:T(4,128)S(1)} %reshape_tile.3, s32[3]{0:T(128)S(1)} %iota_multiply_fusion), kind=kLoop, calls=%fused_computation.62 | loop fusion | flops 81792 | bytes 3084 | tf_op jit(solution)/shard_map/add | solution.py:298
  17.5 2.8 %all-to-all-done = f32[16,24,128]{2,1,0:T(8,128)S(1)} async-done(((f32[16,24,128]{2,1,0:T(8,128)}), f32[16,24,128]{2,1,0:T(8,128)S(1)}, u32[]{:S(2)}, u32[]{:S(2)}) %all-to-all-start) | async-done | bytes 196640 | tf_op jit(solution)/shard_map/all_to_all | solution.py:313
  20.3 0.0 copy-start.1
  20.3 0.7 %copy-done.1 = f32[16,24,128]{2,1,0:T(8,128)} copy-done((f32[16,24,128]{2,1,0:T(8,128)}, f32[16,24,128]{2,1,0:T(8,128)S(1)}, u32[]{:S(2)}) %copy-start.1) | copy-done | bytes 196632
  21.0 2.2 %route.1 = f32[384,128]{1,0:T(8,128)} custom-call(s32[3,128]{1,0:T(4,128)} %fusion.17.index_ref, f32[384,128]{1,0:T(8,128)} %bitcast.20), custom_call_target="tpu_custom_call" | custom-call | tf_op jit(solution)/shard_map/route/pallas_call | solution.py:83
  23.3 3.5 %all-to-all-start.1 = ((f32[16,24,128]{2,1,0:T(8,128)}), f32[16,24,128]{2,1,0:T(8,128)S(1)}, u32[]{:S(2)}, u32[]{:S(2)}) async-start(f32[16,24,128]{2,1,0:T(8,128)} %bitcast.21), calls=%async_computation.1 | async-start | bytes 393216 | tf_op jit(solution)/shard_map/all_to_all | solution.py:319
  26.8 5.1 %inner.3 = (f32[6,8,128,128]{3,2,1,0:T(8,128)}, f32[6,2,8,8,128]{4,3,2,1,0:T(8,128)}) custom-call(f32[6,8,128,128]{3,2,1,0:T(8,128)} %bitcast.13, bf16[6,8,128,128]{3,2,1,0:T(8,128)(2,1)} %bitcast.15, bf16[6,8,128,128]{3,2,1,0:T(8,128)(2,1)} %bitcast.17, bf16[6,8,128,128]{3,2,1,0:T(8,128)(2,1)} %bitcast.19, ...), custom_call_target="tpu_custom_call", output_to_operand_aliasing={{0}: (4, {}), {1}: (5, {})} | custom-call | tf_op jit(solution)/shard_map/inner/pallas_call | solution.py:168
  31.9 3.8 %all-to-all-done.1.refs_3_ = f32[16,24,128]{2,1,0:T(8,128)S(1)} async-done(((f32[16,24,128]{2,1,0:T(8,128)}), f32[16,24,128]{2,1,0:T(8,128)S(1)}, u32[]{:S(2)}, u32[]{:S(2)}) %all-to-all-start.1) | async-done | bytes 196640 | tf_op jit(solution)/shard_map/all_to_all | solution.py:319
  35.7 0.0 copy-start
  35.7 0.7 %copy-done = f32[16,24,128]{2,1,0:T(8,128)} copy-done((f32[16,24,128]{2,1,0:T(8,128)}, f32[16,24,128]{2,1,0:T(8,128)S(1)}, u32[]{:S(2)}) %copy-start) | copy-done | bytes 196632
  36.4 6.5 %edges.1 = f32[6,8,128,128]{3,2,1,0:T(8,128)} custom-call(f32[6,8,128,128]{3,2,1,0:T(8,128)} %get-tuple-element.17.refs_0_, f32[6,2,8,8,128]{4,3,2,1,0:T(8,128)} %get-tuple-element.18.refs_1_, f32[16,24,128]{2,1,0:T(8,128)} %pack.1.refs_2_, f32[16,24,128]{2,1,0:T(8,128)} %copy-done), custom_call_target="tpu_custom_call", output_to_operand_aliasing={{}: (0, {})} | custom-call | tf_op jit(solution)/shard_map/edges/pallas_call | solution.py:242
  (3 shorter events, 0.0 us)
Async XLA Ops:
  0.0 11.4 %copy-start.2 = (s32[6,4,3]{0,1,2:T(4,128)S(1)}, s32[6,4,3]{0,1,2:T(4,128)}, u32[]{:S(2)}) copy-start(s32[6,4,3]{0,1,2:T(4,128)} %param.9) | copy-start | bytes 868
  4.0 16.4 %all-to-all-start = ((f32[16,24,128]{2,1,0:T(8,128)}), f32[16,24,128]{2,1,0:T(8,128)S(1)}, u32[]{:S(2)}, u32[]{:S(2)}) async-start(f32[16,24,128]{2,1,0:T(8,128)} %pack.1.refs_2_), calls=%async_computation | async-start | bytes 393216 | tf_op jit(solution)/shard_map/all_to_all | solution.py:313
  20.3 0.7 %copy-start.1 = (f32[16,24,128]{2,1,0:T(8,128)}, f32[16,24,128]{2,1,0:T(8,128)S(1)}, u32[]{:S(2)}) copy-start(f32[16,24,128]{2,1,0:T(8,128)S(1)} %all-to-all-done) | copy-start | bytes 589828
  23.3 12.5 %all-to-all-start.1 = ((f32[16,24,128]{2,1,0:T(8,128)}), f32[16,24,128]{2,1,0:T(8,128)S(1)}, u32[]{:S(2)}, u32[]{:S(2)}) async-start(f32[16,24,128]{2,1,0:T(8,128)} %bitcast.21), calls=%async_computation.1 | async-start | bytes 393216 | tf_op jit(solution)/shard_map/all_to_all | solution.py:319
  35.7 0.7 %copy-start = (f32[16,24,128]{2,1,0:T(8,128)}, f32[16,24,128]{2,1,0:T(8,128)S(1)}, u32[]{:S(2)}) copy-start(f32[16,24,128]{2,1,0:T(8,128)S(1)} %all-to-all-done.1.refs_3_) | copy-start | bytes 589828

commit v4 on v3

--- a/solution.py
+++ b/solution.py
@@ -9,6 +9,7 @@
 
 DEPTH = 2
 EARLY = 3
+PIECES = 4
 
 
 def split3(x):
@@ -19,13 +20,20 @@
     return hi, mid, low
 
 
-def pack_body(tracer_ref, out_ref, *, count, levels, cells):
+def level_parts(count, levels, cells):
+    shape = (count, levels // PIECES, cells, cells)
+    return [pl.BlockSpec(shape, lambda p, n=n: (p, n, 0, 0)) for n in range(PIECES)]
+
+
+def pack_body(*refs, count, levels, cells):
+    out_ref = refs[-1]
+    part = levels // (len(refs) - 1)
     lane = lax.broadcasted_iota(jnp.int32, (cells, cells), 1)
     group = lane // (2 * DEPTH)
     for p in range(count):
         packed = jnp.zeros((cells, cells), jnp.float32)
         for k in range(levels):
-            turned = pltpu.roll(tracer_ref[p, k], 2 * DEPTH * k + DEPTH, 1)
+            turned = pltpu.roll(refs[k // part][p, k % part], 2 * DEPTH * k + DEPTH, 1)
             packed = jnp.where(group == k, turned, packed)
         rows = packed.T
         for k in range(levels):
@@ -35,22 +43,24 @@
                 north = 2 * DEPTH * k + DEPTH - 1 - d
                 slot = p * 4
                 out_ref[m, slot : slot + 1, :] = rows[south : south + 1]
-                out_ref[m, slot + 1 : slot + 2, :] = tracer_ref[p, k, cells - 1 - d : cells - d, :]
+                out_ref[m, slot + 1 : slot + 2, :] = refs[k // part][
+                    p, k % part, cells - 1 - d : cells - d, :
+                ]
                 out_ref[m, slot + 2 : slot + 3, :] = rows[north : north + 1]
-                out_ref[m, slot + 3 : slot + 4, :] = tracer_ref[p, k, d : d + 1, :]
+                out_ref[m, slot + 3 : slot + 4, :] = refs[k // part][p, k % part, d : d + 1, :]
 
 
 def pack(panels):
     total, levels, cells, _ = panels.shape
     count = 2
     return pl.pallas_call(
-        lambda a, o: pack_body(a, o, count=count, levels=levels, cells=cells),
+        lambda *refs: pack_body(*refs, count=count, levels=levels, cells=cells),
         grid=(total // count,),
-        in_specs=[pl.BlockSpec((count, levels, cells, cells), lambda p: (p, 0, 0, 0))],
+        in_specs=level_parts(count, levels, cells),
         out_specs=pl.BlockSpec((levels * DEPTH, count * 4, cells), lambda p: (0, p, 0)),
         out_shape=jax.ShapeDtypeStruct((levels * DEPTH, total * 4, cells), jnp.float32),
         name="pack",
-    )(panels)
+    )(*[panels] * PIECES)
 
 
 def route_body(index_ref, rows_ref, out_ref):
@@ -183,7 +193,9 @@
     )(panels, east, north, diff, *earlier)
 
 
-def edges_body(inner_ref, lines_ref, own_ref, ghost_ref, out_ref, source_ref, *, levels, cells):
+def edges_body(*refs, levels, cells):
+    lines_ref, own_ref, ghost_ref, out_ref, source_ref = refs[-5:]
+    part = levels // (len(refs) - 5)
     panel = pl.program_id(0)
     lines = 4 * DEPTH
 
@@ -226,7 +238,7 @@
     outer = (lane < DEPTH) | (lane >= cells - DEPTH)
     for k in range(levels):
         moved = pltpu.roll(columns, (cells - DEPTH - k * lines) % cells, 1)
-        value = inner_ref[0, k] + jnp.where(outer, moved, 0.0)
+        value = refs[k // part][0, k % part] + jnp.where(outer, moved, 0.0)
         out_ref[0, k] = value
         out_ref[0, k, 0:DEPTH, :] = value[0:DEPTH] + solved[k][3 * DEPTH :]
         out_ref[0, k, cells - DEPTH : cells, :] = (
@@ -242,8 +254,8 @@
     return pl.pallas_call(
         lambda *refs: edges_body(*refs, levels=levels, cells=cells),
         grid=(count,),
-        in_specs=[
-            block,
+        in_specs=level_parts(1, levels, cells)
+        + [
             pl.BlockSpec((1,) + lines.shape[1:], lambda p: (p, 0, 0, 0, 0)),
             strips,
             strips,
@@ -253,9 +265,8 @@
         scratch_shapes=[
             pltpu.VMEM((levels, 4 * DEPTH, cells), jnp.float32),
         ],
-        input_output_aliases={0: 0},
         name="edges",
-    )(inner_values, lines, own, ghosts)
+    )(*[inner_values] * PIECES, lines, own, ghosts)
 
 
 def row_sources(seam_table, across, cells):

time: 43.5 us -> 43.5 us (level)
  no operation moved by 1% of the time
where the time goes in v4:
time: 43.5 us; the launch traced here: 42.9 us
  Pallas kernels  22.9 us (53%)
  starting transfers between devices  10.9 us (25%)
  waiting for transfers between devices  6.68 us (15%)
  local copies, waits for them, and re-layouts  1.63 us (4%)
  other arithmetic  0.72 us (2%)
    pallas_call x2, Pallas kernels, inner(): pl.pallas_call(lambda *refs: inner_body(*refs, levels=levels, cells=cells...  10.2 us
    all_to_all x1, starting transfers between devices, shards(): held = lax.all_to_all(send, 'tile', 0, 0, tiled=True)  7.43 us
    pallas_call x1, Pallas kernels, edges(): pl.pallas_call(lambda *refs: edges_body(*refs, levels=levels, cells=cells...  6.61 us
    pallas_call x1, Pallas kernels, pack(): pl.pallas_call(lambda *refs: pack_body(*refs, count=count, levels=levels,...  3.87 us
    all_to_all x1, waiting for transfers between devices, shards(): lax.all_to_all(routed.reshape(held.shape), 'tile', 0, 0, tiled=True)  3.84 us
    all_to_all x1, starting transfers between devices, shards(): lax.all_to_all(routed.reshape(held.shape), 'tile', 0, 0, tiled=True)  3.52 us
    all_to_all x1, waiting for transfers between devices, shards(): held = lax.all_to_all(send, 'tile', 0, 0, tiled=True)  2.84 us
    pallas_call x1, Pallas kernels, route(): pl.pallas_call(route_body, out_shape=jax.ShapeDtypeStruct(rows.shape, row...  2.23 us
  transfers between devices with their start and end apart: 2, of which 2 were waited for; matrix products, arithmetic and copies ran while one was open for 2% of the time, Pallas kernels for 24%

profile of v4, /device:TPU:0, one launch (start us, length us, event | category | flops | bytes accessed | tf_op | source)
XLA Modules:
  0.0 42.9 jit_solution(6376533779095984325)
XLA Ops:
  0.0 0.0 copy-start.2
  0.0 3.9 %pack.1.refs_5_ = f32[16,24,128]{2,1,0:T(8,128)} custom-call(f32[6,8,128,128]{3,2,1,0:T(8,128)} %bitcast.11, f32[6,8,128,128]{3,2,1,0:T(8,128)} %bitcast.12, f32[6,8,128,128]{3,2,1,0:T(8,128)} %bitcast.13, f32[6,8,128,128]{3,2,1,0:T(8,128)} %bitcast.14), custom_call_target="tpu_custom_call" | custom-call | tf_op jit(solution)/shard_map/pack/pallas_call | solution.py:56
  3.9 7.4 %all-to-all-start = ((f32[16,24,128]{2,1,0:T(8,128)}), f32[16,24,128]{2,1,0:T(8,128)S(1)}, u32[]{:S(2)}, u32[]{:S(2)}) async-start(f32[16,24,128]{2,1,0:T(8,128)} %pack.1.refs_5_), calls=%async_computation | async-start | bytes 393216 | tf_op jit(solution)/shard_map/all_to_all | solution.py:324
  11.3 0.0 copy-done.2
  11.3 0.1 copy.9
  11.4 0.1 reshape.31
  11.5 0.1 reshape_tile.3
  11.6 5.1 %inner.2 = (f32[6,8,128,128]{3,2,1,0:T(8,128)}, f32[6,2,8,8,128]{4,3,2,1,0:T(8,128)}) custom-call(f32[6,8,128,128]{3,2,1,0:T(8,128)} %bitcast.15, bf16[6,8,128,128]{3,2,1,0:T(8,128)(2,1)} %bitcast.17, bf16[6,8,128,128]{3,2,1,0:T(8,128)(2,1)} %bitcast.19, bf16[6,8,128,128]{3,2,1,0:T(8,128)(2,1)} %bitcast.21), custom_call_target="tpu_custom_call" | custom-call | tf_op jit(solution)/shard_map/inner/pallas_call | solution.py:178
  16.7 0.7 %fusion.17.index_ref = s32[3,128]{1,0:T(4,128)} fusion(s32[3,128]{1,0:T(4,128)S(1)} %reshape_tile.3, s32[3]{0:T(128)S(1)} %iota_multiply_fusion), kind=kLoop, calls=%fused_computation.62 | loop fusion | flops 81792 | bytes 3084 | tf_op jit(solution)/shard_map/add | solution.py:309
  17.4 2.8 %all-to-all-done = f32[16,24,128]{2,1,0:T(8,128)S(1)} async-done(((f32[16,24,128]{2,1,0:T(8,128)}), f32[16,24,128]{2,1,0:T(8,128)S(1)}, u32[]{:S(2)}, u32[]{:S(2)}) %all-to-all-start) | async-done | bytes 196640 | tf_op jit(solution)/shard_map/all_to_all | solution.py:324
  20.3 0.0 copy-start.1
  20.3 0.7 %copy-done.1 = f32[16,24,128]{2,1,0:T(8,128)} copy-done((f32[16,24,128]{2,1,0:T(8,128)}, f32[16,24,128]{2,1,0:T(8,128)S(1)}, u32[]{:S(2)}) %copy-start.1) | copy-done | bytes 196632
  20.9 2.2 %route.1 = f32[384,128]{1,0:T(8,128)} custom-call(s32[3,128]{1,0:T(4,128)} %fusion.17.index_ref, f32[384,128]{1,0:T(8,128)} %bitcast.23), custom_call_target="tpu_custom_call" | custom-call | tf_op jit(solution)/shard_map/route/pallas_call | solution.py:93
  23.2 3.5 %all-to-all-start.1 = ((f32[16,24,128]{2,1,0:T(8,128)}), f32[16,24,128]{2,1,0:T(8,128)S(1)}, u32[]{:S(2)}, u32[]{:S(2)}) async-start(f32[16,24,128]{2,1,0:T(8,128)} %bitcast.24), calls=%async_computation.1 | async-start | bytes 393216 | tf_op jit(solution)/shard_map/all_to_all | solution.py:330
  26.7 5.1 %inner.3 = (f32[6,8,128,128]{3,2,1,0:T(8,128)}, f32[6,2,8,8,128]{4,3,2,1,0:T(8,128)}) custom-call(f32[6,8,128,128]{3,2,1,0:T(8,128)} %bitcast.16, bf16[6,8,128,128]{3,2,1,0:T(8,128)(2,1)} %bitcast.18, bf16[6,8,128,128]{3,2,1,0:T(8,128)(2,1)} %bitcast.20, bf16[6,8,128,128]{3,2,1,0:T(8,128)(2,1)} %bitcast.22, ...), custom_call_target="tpu_custom_call", output_to_operand_aliasing={{0}: (4, {}), {1}: (5, {})} | custom-call | tf_op jit(solution)/shard_map/inner/pallas_call | solution.py:178
  31.8 3.8 %all-to-all-done.1.refs_6_ = f32[16,24,128]{2,1,0:T(8,128)S(1)} async-done(((f32[16,24,128]{2,1,0:T(8,128)}), f32[16,24,128]{2,1,0:T(8,128)S(1)}, u32[]{:S(2)}, u32[]{:S(2)}) %all-to-all-start.1) | async-done | bytes 196640 | tf_op jit(solution)/shard_map/all_to_all | solution.py:330
  35.6 0.0 copy-start
  35.6 0.7 %copy-done = f32[16,24,128]{2,1,0:T(8,128)} copy-done((f32[16,24,128]{2,1,0:T(8,128)}, f32[16,24,128]{2,1,0:T(8,128)S(1)}, u32[]{:S(2)}) %copy-start) | copy-done | bytes 196632
  36.3 6.6 %edges.1 = f32[6,8,128,128]{3,2,1,0:T(8,128)} custom-call(f32[6,8,128,128]{3,2,1,0:T(8,128)} %get-tuple-element.17.refs_0_.refs_1_.refs_2_.refs_3_, f32[6,8,128,128]{3,2,1,0:T(8,128)} %get-tuple-element.17.refs_0_.refs_1_.refs_2_.refs_3_, f32[6,8,128,128]{3,2,1,0:T(8,128)} %get-tuple-element.17.refs_0_.refs_1_.refs_2_.refs_3_, ...), custom_call_target="tpu_custom_call" | custom-call | tf_op jit(solution)/shard_map/edges/pallas_call | solution.py:254
  (3 shorter events, 0.0 us)
Async XLA Ops:
  0.0 11.3 %copy-start.2 = (s32[6,4,3]{0,1,2:T(4,128)S(1)}, s32[6,4,3]{0,1,2:T(4,128)}, u32[]{:S(2)}) copy-start(s32[6,4,3]{0,1,2:T(4,128)} %param.9) | copy-start | bytes 868
  3.9 16.4 %all-to-all-start = ((f32[16,24,128]{2,1,0:T(8,128)}), f32[16,24,128]{2,1,0:T(8,128)S(1)}, u32[]{:S(2)}, u32[]{:S(2)}) async-start(f32[16,24,128]{2,1,0:T(8,128)} %pack.1.refs_5_), calls=%async_computation | async-start | bytes 393216 | tf_op jit(solution)/shard_map/all_to_all | solution.py:324
  20.3 0.7 %copy-start.1 = (f32[16,24,128]{2,1,0:T(8,128)}, f32[16,24,128]{2,1,0:T(8,128)S(1)}, u32[]{:S(2)}) copy-start(f32[16,24,128]{2,1,0:T(8,128)S(1)} %all-to-all-done) | copy-start | bytes 589828
  23.2 12.5 %all-to-all-start.1 = ((f32[16,24,128]{2,1,0:T(8,128)}), f32[16,24,128]{2,1,0:T(8,128)S(1)}, u32[]{:S(2)}, u32[]{:S(2)}) async-start(f32[16,24,128]{2,1,0:T(8,128)} %bitcast.24), calls=%async_computation.1 | async-start | bytes 393216 | tf_op jit(solution)/shard_map/all_to_all | solution.py:330
  35.6 0.7 %copy-start = (f32[16,24,128]{2,1,0:T(8,128)}, f32[16,24,128]{2,1,0:T(8,128)S(1)}, u32[]{:S(2)}) copy-start(f32[16,24,128]{2,1,0:T(8,128)S(1)} %all-to-all-done.1.refs_6_) | copy-start | bytes 589828
